TPU v7x, 512 devices: a whole 4x4x16 slice. The times are simulated.
512 devices in a mesh: dom: 64 (over x_lo, z, core), orb: 8 (over y, x_hi).
Axes of the slice: x: 4 (x_hi: 2, x_lo: 2; x = x_hi * 2 + x_lo), y: 4, z: 16, core: 2. Of those that a mesh axis runs over, the one named last changes fastest.
Arguments:
- orbitals: bfloat16 [16, 256, 256, 128], P('orb', 'dom'), may hold values from -2.390625 to 2.390625
- energies: float32 [16], P('orb'), may hold values from -1.5 to -0.3
- local_potential: float32 [256, 256, 128], P('dom'), may hold values from -4 to 4
- lanczos: bfloat16 [16, 256, 256, 128], P('orb', 'dom'), may hold values from -40 to 40
- previous: bfloat16 [16, 256, 256, 128], P('orb', 'dom'), may hold values from -6 to 6
- beta: float32 [1], replicated, may hold values from 0.3 to 1.5
Outputs:
- next_vector: bfloat16 [16, 256, 256, 128], P('orb', 'dom')
- alpha: float32 [1], replicated
- beta_next: float32 [1], replicated
All inputs are finite; a program needn't handle non-finite values.
Results may differ from a plain program's by a relative error of at most 0.0085.
Values may be sent and summed in bfloat16 or wider, within the bound.
A program may use at most 64 MiB of HBM per device.

v0:
```python
import jax
import jax.numpy as jnp
from jax import lax
from jax.sharding import Mesh
from jax.sharding import PartitionSpec as P

DOM = ("dom_0", "dom_1", "dom_2")
ORB = ("orb_0", "orb_1")
DOM_ORB = ("dom_0", "dom_1", "dom_2", "orb_0", "orb_1")


side_weights = (1.5, -0.15, 1.0 / 90.0)
central_weight = -49.0 / 18.0
screening = 1.0 / 64.0


def extended(array, sides, width):
    for axis, dim in sides:
        size, length = (lax.axis_size(axis), array.shape[dim])
        up = [(i, (i + 1) % size) for i in range(size)]
        down = [(j, i) for i, j in up]
        last = lax.slice_in_dim(array, length - width, length, axis=dim)
        first = lax.slice_in_dim(array, 0, width, axis=dim)
        before = lax.ppermute(last, axis, up)
        after = lax.ppermute(first, axis, down)
        array = jnp.concatenate([before, array, after], axis=dim)
    return array


def cut_along(array, dim, size):
    before, after = (array.shape[:dim], array.shape[dim + 1 :])
    return jnp.moveaxis(array.reshape(*before, size, -1, *after), dim, 0)


def sent_and_summed(array, axis, dim):
    parts = cut_along(array, dim, lax.axis_size(axis))
    arrived = lax.all_to_all(parts, axis, split_axis=0, concat_axis=0, tiled=True)
    return arrived.sum(axis=0)


def in_order(parts, dim):
    lengths = list(parts.shape[1:])
    lengths[dim] *= parts.shape[0]
    return jnp.moveaxis(parts, 0, dim).reshape(lengths)


def from_everyone(array, axis):
    copies = jnp.broadcast_to(array, (lax.axis_size(axis), *array.shape))
    return lax.all_to_all(copies, axis, split_axis=0, concat_axis=0, tiled=True)


def collect(array, axis, dim):
    return in_order(from_everyone(array, axis), dim)


def over_axes(array, axes):
    for axis in axes:
        array = lax.psum(array, axis)
    return array


def cas_table(length):
    position = jnp.arange(length, dtype=jnp.int32)
    phase = position[:, None] * position[None, :] % length
    angle = 2.0 * jnp.pi / length * phase.astype(jnp.float32)
    return jnp.cos(angle) + jnp.sin(angle)


def wave_square(position, length):
    folded = jnp.minimum(position, length - position).astype(jnp.float32)
    wavenumber = 2.0 * jnp.pi / length * folded
    return wavenumber * wavenumber


def transform_lateral(values):
    highest = lax.Precision.HIGHEST
    result = jnp.einsum("by,ayz->abz", cas_table(values.shape[1]), values, precision=highest)
    return jnp.einsum("cz,abz->abc", cas_table(values.shape[2]), result, precision=highest)


def per_device(orbitals, energies, local_potential, lanczos, previous, beta):
    highest = lax.Precision.HIGHEST
    planes = lanczos.shape[1]
    length_y = lanczos.shape[2]
    length_z = lanczos.shape[3]
    length_x = planes * lax.axis_size(DOM)
    normalizer = 4.0 * jnp.pi / (length_x * length_y * length_z)
    padded = extended(lanczos, ((DOM, 1),), 3).astype(jnp.float32)
    current = padded[:, 3 : 3 + planes]
    laplace = 3.0 * central_weight * current
    for offset, weight in enumerate(side_weights):
        reach = offset + 1
        laplace = laplace + weight * (
            padded[:, 3 + reach : 3 + reach + planes] + padded[:, 3 - reach : 3 - reach + planes]
        )
        for dimension in (2, 3):
            laplace = laplace + weight * (
                jnp.roll(current, reach, dimension) + jnp.roll(current, -reach, dimension)
            )
    partial_density = jnp.sum(orbitals.astype(jnp.float32) * current, axis=0)
    square_x = wave_square(jnp.arange(length_x, dtype=jnp.int32), length_x)
    table_x = cas_table(length_x)
    shared = sent_and_summed(transform_lateral(partial_density), ORB, 1)
    band_rows = shared.shape[1]
    flattened = shared.reshape(planes, band_rows * length_z)
    columns = lax.all_to_all(flattened, DOM, split_axis=1, concat_axis=0, tiled=True)
    column_count = columns.shape[1]
    column_index = lax.axis_index(DOM) * column_count + jnp.arange(column_count, dtype=jnp.int32)
    index_y = lax.axis_index(ORB) * band_rows + column_index // length_z
    index_z = column_index % length_z
    square_rest = wave_square(index_y, length_y) + wave_square(index_z, length_z)
    summed = square_x[:, None] + square_rest[None, :] + screening
    columns = jnp.einsum("ax,xc->ac", table_x, columns, precision=highest) * (normalizer / summed)
    columns = jnp.einsum("ax,xc->ac", table_x, columns, precision=highest)
    flattened = lax.all_to_all(
        columns.astype(jnp.bfloat16), DOM, split_axis=0, concat_axis=1, tiled=True
    ).astype(columns.dtype)
    shared = flattened.reshape(planes, band_rows, length_z)
    potential = transform_lateral(collect(shared.astype(jnp.bfloat16), ORB, 1).astype(shared.dtype))
    image = -0.5 * laplace + (local_potential[None] - energies[:, None, None, None]) * current
    image = image + orbitals.astype(jnp.float32) * potential[None]
    entries = float(lanczos.shape[0] * lax.axis_size(ORB) * length_x * length_y * length_z)
    older = previous.astype(jnp.float32)
    beta_now = beta[0]
    moments = (
        over_axes(jnp.sum(current * image), DOM_ORB),
        over_axes(jnp.sum(image * image), DOM_ORB),
        over_axes(jnp.sum(older * image), DOM_ORB),
        over_axes(jnp.sum(current * current), DOM_ORB),
        over_axes(jnp.sum(current * older), DOM_ORB),
        over_axes(jnp.sum(older * older), DOM_ORB),
    )
    cross_mean = moments[0] / entries
    image_mean = moments[1] / entries
    older_image = moments[2] / entries
    self_mean = moments[3] / entries
    mixed_mean = moments[4] / entries
    older_mean = moments[5] / entries
    squares = image_mean - 2.0 * cross_mean * cross_mean - 2.0 * beta_now * older_image
    squares = (
        squares + cross_mean * cross_mean * self_mean + 2.0 * cross_mean * beta_now * mixed_mean
    )
    squares = squares + beta_now * beta_now * older_mean
    remainder = image - cross_mean * current - beta_now * older
    norm_next = jnp.sqrt(squares + 1e-06)
    next_vector = (remainder / norm_next).astype(jnp.bfloat16)
    return (next_vector, jnp.reshape(cross_mean, (1,)), jnp.reshape(norm_next, (1,)))


def solution(mesh):
    finer = Mesh(
        mesh.devices.reshape(2, 16, 2, 4, 2), ("dom_0", "dom_1", "dom_2", "orb_0", "orb_1")
    )
    placed = (
        P(ORB, DOM, None, None),
        P(ORB),
        P(DOM, None, None),
        P(ORB, DOM, None, None),
        P(ORB, DOM, None, None),
        P(),
    )
    return jax.shard_map(
        per_device,
        mesh=finer,
        in_specs=placed,
        out_specs=(P(ORB, DOM, None, None), P(), P()),
        check_vma=False,
    )
```

profile of v0, /device:TPU:1, one launch (start us, length us, event | category | flops | bytes accessed | tf_op | source)
XLA Modules:
  0.0 202.7 jit_solution(14370648942303184739)
XLA Ops:
  0.6 1.2 fusion.90
  1.8 4.9 %collective-permute-start = (bf16[2,3,256,128]{3,2,1,0:T(8,128)(2,1)S(1)}, bf16[2,3,256,128]{3,2,1,0:T(8,128)(2,1)S(1)}, u32[]{:S(2)}, u32[]{:S(2)}) collective-permute-start(bf16[2,3,256,128]{3,2,1,0:T(8,128)(2,1)S(1)} %get-tuple-element.65), channel_id=1, source_target_pairs={{0,8},{8,16},{16,24},{24,32},{32,40},{40,48},{48,56},{56,64},{64,7... | collective-permute-start | bytes 1179656 | tf_op jit(solution)/shard_map/ppermute | solution.py:24
  6.7 5.7 %collective-permute-start.1 = (bf16[2,3,256,128]{3,2,1,0:T(8,128)(2,1)S(1)}, bf16[2,3,256,128]{3,2,1,0:T(8,128)(2,1)S(1)}, u32[]{:S(2)}, u32[]{:S(2)}) collective-permute-start(bf16[2,3,256,128]{3,2,1,0:T(8,128)(2,1)S(1)} %get-tuple-element.66), channel_id=1, source_target_pairs={{8,0},{16,8},{24,16},{32,24},{40,32},{48,40},{56,48},{64,56},{72,6... | collective-permute-start | bytes 1179656 | tf_op jit(solution)/shard_map/ppermute | solution.py:25
  13.2 2.9 %collective-permute-done.1 = bf16[2,3,256,128]{3,2,1,0:T(8,128)(2,1)S(1)} collective-permute-done((bf16[2,3,256,128]{3,2,1,0:T(8,128)(2,1)S(1)}, bf16[2,3,256,128]{3,2,1,0:T(8,128)(2,1)S(1)}, u32[]{:S(2)}, u32[]{:S(2)}) %collective-permute-start.1) | collective-permute-done | bytes 393248 | tf_op jit(solution)/shard_map/ppermute | solution.py:25
  16.1 1.4 maximum_convert_fusion
  17.5 1.4 fusion.81
  19.0 1.7 fusion.82
  20.6 1.7 fusion.83
  22.3 1.5 fusion.84
  23.8 1.7 fusion.85
  25.5 1.0 fusion.6
  26.5 1.9 convolution_bitcast_fusion.1
  28.4 1.1 fusion.41
  29.5 0.8 copy.32
  30.4 6.8 %all-to-all-start = ((f32[8,4,32,128]{3,2,1,0:T(8,128)}), f32[8,4,32,128]{3,2,1,0:T(8,128)}, u32[]{:S(2)}, u32[]{:S(2)}) async-start(f32[8,4,32,128]{3,2,1,0:T(8,128)} %bitcast.44), calls=%async_computation | async-start | bytes 1048576 | tf_op jit(solution)/shard_map/all_to_all | solution.py:37
  37.1 1.6 fusion.86
  39.4 1.6 fusion.87
  41.0 5.3 %all-to-all-done = f32[8,4,32,128]{3,2,1,0:T(8,128)} async-done(((f32[8,4,32,128]{3,2,1,0:T(8,128)}), f32[8,4,32,128]{3,2,1,0:T(8,128)}, u32[]{:S(2)}, u32[]{:S(2)}) %all-to-all-start) | async-done | bytes 524320 | tf_op jit(solution)/shard_map/all_to_all | solution.py:37
  46.3 1.7 reduce_sum.73
  48.0 1.6 all_to_all.35
  49.6 1.7 copy.33
  51.2 1.7 reshape.88
  52.9 18.2 %all-to-all-start.1 = ((f32[64,1,256]{2,1,0:T(1,128)}), f32[64,1,256]{2,1,0:T(1,128)}, u32[]{:S(2)}, u32[]{:S(2)}) async-start(f32[64,1,256]{2,1,0:T(1,128)} %reshape.88), calls=%async_computation.1 | async-start | bytes 131072 | tf_op jit(solution)/shard_map/all_to_all | solution.py:106
  71.1 1.7 fusion.88
  72.7 12.8 %all-to-all-done.1 = f32[64,1,256]{2,1,0:T(1,128)} async-done(((f32[64,1,256]{2,1,0:T(1,128)}), f32[64,1,256]{2,1,0:T(1,128)}, u32[]{:S(2)}, u32[]{:S(2)}) %all-to-all-start.1) | async-done | bytes 65568 | tf_op jit(solution)/shard_map/all_to_all | solution.py:106
  86.1 2.3 %reduce = f32[64,256]{1,0:T(8,128)} reduce(f32[64,1,256]{2,1,0:T(1,128)} %all-to-all-done.1, f32[]{:T(128)} %broadcast.167), dimensions={1}, to_apply=%all_to_all.36.reduce_sub_computation | reduce | bytes 131076 | tf_op jit(solution)/shard_map/all_to_all | solution.py:106
  88.3 1.6 reshape.89
  89.9 2.3 %convolution_multiply_fusion = f32[256,64]{0,1:T(8,128)S(1)} fusion(f32[256,64]{1,0:T(8,128)} %bitcast.50, f32[64]{0:T(128)S(1)} %fusion.52, f32[256]{0:T(256)S(1)} %fusion.48), kind=kOutput, calls=%fused_computation.9 | convolution fusion | flops 51380224 | bytes 132352 | tf_op jit(solution)/shard_map/ax,xc->ac/dot_general | solution.py:113
  92.2 2.2 %convolution_convert_fusion = bf16[256,64]{0,1:T(8,128)(2,1)} fusion(f32[256,64]{0,1:T(8,128)S(1)} %convolution_multiply_fusion), kind=kOutput, calls=%fused_computation.10 | convolution fusion | flops 51331072 | bytes 98304 | tf_op jit(solution)/shard_map/ax,xc->ac/dot_general | solution.py:114
  94.5 1.5 copy.21
  96.0 1.5 reshape.90
  97.5 5.2 %all-to-all-start.2 = ((bf16[64,2,128]{2,1,0:T(2,128)(2,1)}), bf16[64,2,128]{2,1,0:T(2,128)(2,1)}, u32[]{:S(2)}, u32[]{:S(2)}) async-start(bf16[64,2,128]{2,1,0:T(2,128)(2,1)} %reshape.90), calls=%async_computation.2 | async-start | bytes 65536 | tf_op jit(solution)/shard_map/all_to_all | solution.py:115
  102.7 0.6 maximum_convert_fusion.6
  103.9 12.1 %all-to-all-done.2 = bf16[64,2,128]{2,1,0:T(2,128)(2,1)} async-done(((bf16[64,2,128]{2,1,0:T(2,128)(2,1)}), bf16[64,2,128]{2,1,0:T(2,128)(2,1)}, u32[]{:S(2)}, u32[]{:S(2)}) %all-to-all-start.2) | async-done | bytes 32800 | tf_op jit(solution)/shard_map/all_to_all | solution.py:115
  116.0 0.8 reshape.91
  117.0 0.7 broadcast_in_dim.2
  117.7 3.6 %all-to-all-start.3 = ((bf16[8,4,32,128]{3,2,1,0:T(8,128)(2,1)}), bf16[8,4,32,128]{3,2,1,0:T(8,128)(2,1)S(1)}, u32[]{:S(2)}, u32[]{:S(2)}) async-start(bf16[8,4,32,128]{3,2,1,0:T(8,128)(2,1)} %broadcast_in_dim.2), calls=%async_computation.3 | async-start | bytes 524288 | tf_op jit(solution)/shard_map/all_to_all | solution.py:49
  121.4 1.7 fusion.89
  123.1 6.5 %all-to-all-done.3 = bf16[8,4,32,128]{3,2,1,0:T(8,128)(2,1)S(1)} async-done(((bf16[8,4,32,128]{3,2,1,0:T(8,128)(2,1)}), bf16[8,4,32,128]{3,2,1,0:T(8,128)(2,1)S(1)}, u32[]{:S(2)}, u32[]{:S(2)}) %all-to-all-start.3) | async-done | bytes 262176 | tf_op jit(solution)/shard_map/all_to_all | solution.py:49
  129.6 1.5 convolution_bitcast_fusion
  131.1 1.1 fusion.39
  132.3 9.1 %fusion.5 = (f32[]{:T(128)}, f32[]{:T(128)}, f32[]{:T(128)}, f32[]{:T(128)}, f32[2,4,256,128]{3,2,1,0:T(8,128)}) fusion(bf16[2,4,256,128]{3,2,1,0:T(8,128)(2,1)S(1)} %copy-done.4, f32[2,10,256,128]{3,2,1,0:T(8,128)S(1)} %maximum_convert_fusion, f32[4,256,128]{2,1,0:T(8,128)S(1)} %fusion.39, bf16[2,4,256,128]{3,2,1,0:T(8,128)(2,1)S(1)} %copy-done.8, ...), kind=kLoop, calls=%fused_computation.16 | loop fusion | flops 14680060 | bytes 23068696 | tf_op jit(solution)/shard_map/reduce_sum | solution.py:128
  141.4 4.5 %all-reduce.4 = (f32[]{:T(128)}, f32[]{:T(128)}, f32[]{:T(128)}, f32[]{:T(128)}, f32[]{:T(128)}, /*index=5*/f32[]{:T(128)}) all-reduce(f32[]{:T(128)} %get-tuple-element.7, f32[]{:T(128)} %get-tuple-element.8, f32[]{:T(128)} %get-tuple-element.6, ...), channel_id=1, replica_groups=mesh['dom_0'=2,'dom_1'=16,'dom_2'=2,'orb_0'=4,'orb_1'=2] {'dom_0'}, use_global_device_ids=true, to_apply=%region_9.10 | all-reduce | flops 6 | bytes 48 | tf_op jit(solution)/shard_map/psum | solution.py:58
  145.9 20.9 %all-reduce = (f32[]{:T(128)}, f32[]{:T(128)}, f32[]{:T(128)}, f32[]{:T(128)}, f32[]{:T(128)}, /*index=5*/f32[]{:T(128)}) all-reduce(f32[]{:T(128)} %get-tuple-element.34, f32[]{:T(128)} %get-tuple-element.35, f32[]{:T(128)} %get-tuple-element.36, ...), channel_id=1, replica_groups=mesh['dom_0'=2,'dom_1'=16,'dom_2'=2,'orb_0'=4,'orb_1'=2] {'dom_1'}, use_global_device_ids=true, to_apply=%region_10.11 | all-reduce | flops 6 | bytes 48 | tf_op jit(solution)/shard_map/psum | solution.py:58
  166.8 12.5 %all-reduce.3 = (f32[]{:T(128)}, f32[]{:T(128)}, f32[]{:T(128)}, f32[]{:T(128)}, f32[]{:T(128)}, /*index=5*/f32[]{:T(128)}) all-reduce(f32[]{:T(128)} %get-tuple-element.10, f32[]{:T(128)} %get-tuple-element.11, f32[]{:T(128)} %get-tuple-element.12, ...), channel_id=1, replica_groups=mesh['dom_0'=2,'dom_1'=16,'dom_2'=2,'orb_0'=4,'orb_1'=2] {'dom_2'}, use_global_device_ids=true, to_apply=%region_11.12 | all-reduce | flops 6 | bytes 48 | tf_op jit(solution)/shard_map/psum | solution.py:58
  179.3 7.2 %all-reduce.1 = (f32[]{:T(128)}, f32[]{:T(128)}, f32[]{:T(128)}, f32[]{:T(128)}, f32[]{:T(128)}, /*index=5*/f32[]{:T(128)}) all-reduce(f32[]{:T(128)} %get-tuple-element.28, f32[]{:T(128)} %get-tuple-element.29, f32[]{:T(128)} %get-tuple-element.30, ...), channel_id=1, replica_groups=mesh['dom_0'=2,'dom_1'=16,'dom_2'=2,'orb_0'=4,'orb_1'=2] {'orb_0'}, use_global_device_ids=true, to_apply=%region_12.13 | all-reduce | flops 6 | bytes 48 | tf_op jit(solution)/shard_map/psum | solution.py:58
  186.6 6.0 %all-reduce.2 = (f32[]{:T(128)}, f32[]{:T(128)}, f32[]{:T(128)}, f32[]{:T(128)}, f32[]{:T(128)}, /*index=5*/f32[]{:T(128)}) all-reduce(f32[]{:T(128)} %get-tuple-element.16, f32[]{:T(128)} %get-tuple-element.17, f32[]{:T(128)} %get-tuple-element.18, ...), channel_id=1, replica_groups=mesh['dom_0'=2,'dom_1'=16,'dom_2'=2,'orb_0'=4,'orb_1'=2] {'orb_1'}, use_global_device_ids=true, to_apply=%region_13.14 | all-reduce | flops 6 | bytes 48 | tf_op jit(solution)/shard_map/psum | solution.py:58
  198.2 2.3 %fusion.4 = bf16[2,4,256,128]{3,2,1,0:T(8,128)(2,1)} fusion(bf16[2,4,256,128]{3,2,1,0:T(8,128)(2,1)S(1)} %copy-done.4, f32[2,4,256,128]{3,2,1,0:T(8,128)} %get-tuple-element.40, f32[2,10,256,128]{3,2,1,0:T(8,128)S(1)} %maximum_convert_fusion, f32[]{:T(128)} %sqrt.3, f32[]{:T(128)} %bitcast.39, f32[]{:T(128)} %div.44), kind=kLoop, calls=%fused_computation.15 | loop fusion | flops 1835008 | bytes 3145740 | tf_op jit(solution)/shard_map/convert_element_type | solution.py:146
  (39 shorter events, 2.0 us)
Async XLA Ops:
  1.8 11.4 %collective-permute-start = (bf16[2,3,256,128]{3,2,1,0:T(8,128)(2,1)S(1)}, bf16[2,3,256,128]{3,2,1,0:T(8,128)(2,1)S(1)}, u32[]{:S(2)}, u32[]{:S(2)}) collective-permute-start(bf16[2,3,256,128]{3,2,1,0:T(8,128)(2,1)S(1)} %get-tuple-element.65), channel_id=1, source_target_pairs={{0,8},{8,16},{16,24},{24,32},{32,40},{40,48},{48,56},{56,64},{64,7... | collective-permute-start | bytes 1179656 | tf_op jit(solution)/shard_map/ppermute | solution.py:24
  6.7 9.4 %collective-permute-start.1 = (bf16[2,3,256,128]{3,2,1,0:T(8,128)(2,1)S(1)}, bf16[2,3,256,128]{3,2,1,0:T(8,128)(2,1)S(1)}, u32[]{:S(2)}, u32[]{:S(2)}) collective-permute-start(bf16[2,3,256,128]{3,2,1,0:T(8,128)(2,1)S(1)} %get-tuple-element.66), channel_id=1, source_target_pairs={{8,0},{16,8},{24,16},{32,24},{40,32},{48,40},{56,48},{64,56},{72,6... | collective-permute-start | bytes 1179656 | tf_op jit(solution)/shard_map/ppermute | solution.py:25
  16.1 2.8 %copy-start.1 = (bf16[2,3,256,128]{3,2,1,0:T(8,128)(2,1)}, bf16[2,3,256,128]{3,2,1,0:T(8,128)(2,1)S(1)}, u32[]{:S(2)}) copy-start(bf16[2,3,256,128]{3,2,1,0:T(8,128)(2,1)S(1)} %collective-permute-done.1) | copy-start | bytes 1179652
  23.8 1.7 copy-start.3
  23.8 1.7 copy-start.7
  30.4 8.4 %copy-start = (bf16[2,4,256,128]{3,2,1,0:T(8,128)(2,1)S(1)}, bf16[2,4,256,128]{3,2,1,0:T(8,128)(2,1)}, u32[]{:S(2)}) copy-start(bf16[2,4,256,128]{3,2,1,0:T(8,128)(2,1)} %param.9) | copy-start | bytes 1572868
  30.4 15.9 %all-to-all-start = ((f32[8,4,32,128]{3,2,1,0:T(8,128)}), f32[8,4,32,128]{3,2,1,0:T(8,128)}, u32[]{:S(2)}, u32[]{:S(2)}) async-start(f32[8,4,32,128]{3,2,1,0:T(8,128)} %bitcast.44), calls=%async_computation | async-start | bytes 1048576 | tf_op jit(solution)/shard_map/all_to_all | solution.py:37
  37.1 1.7 copy-start.2
  52.9 32.7 %all-to-all-start.1 = ((f32[64,1,256]{2,1,0:T(1,128)}), f32[64,1,256]{2,1,0:T(1,128)}, u32[]{:S(2)}, u32[]{:S(2)}) async-start(f32[64,1,256]{2,1,0:T(1,128)} %reshape.88), calls=%async_computation.1 | async-start | bytes 131072 | tf_op jit(solution)/shard_map/all_to_all | solution.py:106
  97.5 18.5 %all-to-all-start.2 = ((bf16[64,2,128]{2,1,0:T(2,128)(2,1)}), bf16[64,2,128]{2,1,0:T(2,128)(2,1)}, u32[]{:S(2)}, u32[]{:S(2)}) async-start(bf16[64,2,128]{2,1,0:T(2,128)(2,1)} %reshape.90), calls=%async_computation.2 | async-start | bytes 65536 | tf_op jit(solution)/shard_map/all_to_all | solution.py:115
  117.7 11.8 %all-to-all-start.3 = ((bf16[8,4,32,128]{3,2,1,0:T(8,128)(2,1)}), bf16[8,4,32,128]{3,2,1,0:T(8,128)(2,1)S(1)}, u32[]{:S(2)}, u32[]{:S(2)}) async-start(bf16[8,4,32,128]{3,2,1,0:T(8,128)(2,1)} %broadcast_in_dim.2), calls=%async_computation.3 | async-start | bytes 524288 | tf_op jit(solution)/shard_map/all_to_all | solution.py:49
  121.3 10.9 %copy-start.4 = (bf16[2,4,256,128]{3,2,1,0:T(8,128)(2,1)S(1)}, bf16[2,4,256,128]{3,2,1,0:T(8,128)(2,1)}, u32[]{:S(2)}) copy-start(bf16[2,4,256,128]{3,2,1,0:T(8,128)(2,1)} %param.10) | copy-start | bytes 1572868
  121.4 10.9 %copy-start.9 = (f32[2,4,3,128]{3,2,1,0:T(4,128)S(1)}, f32[2,4,3,128]{3,2,1,0:T(4,128)}, u32[]{:S(2)}) copy-start(f32[2,4,3,128]{3,2,1,0:T(4,128)} %get-tuple-element.64) | copy-start | bytes 36868
  121.4 10.9 %copy-start.10 = (f32[2,4,2,128]{3,2,1,0:T(2,128)S(1)}, f32[2,4,2,128]{3,2,1,0:T(2,128)}, u32[]{:S(2)}) copy-start(f32[2,4,2,128]{3,2,1,0:T(2,128)} %get-tuple-element.61) | copy-start | bytes 24580
  121.4 10.9 %copy-start.11 = (f32[2,4,2,128]{3,2,1,0:T(2,128)S(1)}, f32[2,4,2,128]{3,2,1,0:T(2,128)}, u32[]{:S(2)}) copy-start(f32[2,4,2,128]{3,2,1,0:T(2,128)} %get-tuple-element.62) | copy-start | bytes 24580
  121.4 10.9 %copy-start.12 = (f32[2,4,1,128]{3,2,1,0:T(1,128)S(1)}, f32[2,4,1,128]{3,2,1,0:T(1,128)}, u32[]{:S(2)}) copy-start(f32[2,4,1,128]{3,2,1,0:T(1,128)} %get-tuple-element.59) | copy-start | bytes 12292
  121.4 10.9 %copy-start.13 = (f32[2,4,1,128]{3,2,1,0:T(1,128)S(1)}, f32[2,4,1,128]{3,2,1,0:T(1,128)}, u32[]{:S(2)}) copy-start(f32[2,4,1,128]{3,2,1,0:T(1,128)} %get-tuple-element.60) | copy-start | bytes 12292
  121.4 10.9 %copy-start.14 = (f32[2]{0:T(128)S(1)}, f32[2]{0:T(128)}, u32[]{:S(2)}) copy-start(f32[2]{0:T(128)} %param.7) | copy-start | bytes 28
  129.5 2.7 %copy-start.5 = (f32[2,4,255,128]{3,2,1,0:T(8,128)S(1)}, f32[2,4,255,128]{3,2,1,0:T(8,128)}, u32[]{:S(2)}) copy-start(f32[2,4,255,128]{3,2,1,0:T(8,128)} %get-tuple-element.41) | copy-start | bytes 3133444
  129.5 2.7 %copy-start.6 = (f32[2,4,255,128]{3,2,1,0:T(8,128)S(1)}, f32[2,4,255,128]{3,2,1,0:T(8,128)}, u32[]{:S(2)}) copy-start(f32[2,4,255,128]{3,2,1,0:T(8,128)} %get-tuple-element.42) | copy-start | bytes 3133444
  129.5 2.8 %copy-start.8 = (bf16[2,4,256,128]{3,2,1,0:T(8,128)(2,1)S(1)}, bf16[2,4,256,128]{3,2,1,0:T(8,128)(2,1)}, u32[]{:S(2)}) copy-start(bf16[2,4,256,128]{3,2,1,0:T(8,128)(2,1)} %param.6) | copy-start | bytes 1572868
where the time goes:
time: 206 us; the launch traced here: 203 us
  blocking collectives  51.1 us (25%)
  starting transfers between devices  44.4 us (22%)
  waiting for transfers between devices  39.6 us (19%)
  local copies, waits for them, and re-layouts  28.4 us (14%)
  other arithmetic  19.5 us (9%)
  matrix products  10.2 us (5%)
  between operations  9.51 us (5%)
    psum x5, blocking collectives, over_axes(): array = lax.psum(array, axis)  51.1 us
    all_to_all x1, starting transfers between devices, per_device(): lax.all_to_all(flattened, DOM, split_axis=1, concat_axis=0, tiled=True)  18.2 us
    slice x9, local copies, waits for them, and re-layouts, per_device(): jnp.roll(current, reach, dimension) + jnp.roll(current, -reach, dimension)  14.5 us
    all_to_all x1, waiting for transfers between devices, per_device(): lax.all_to_all(flattened, DOM, split_axis=1, concat_axis=0, tiled=True)  12.8 us
    all_to_all x1, waiting for transfers between devices, per_device(): lax.all_to_all(columns.astype(jnp.bfloat16), DOM, split_axis=0, concat_ax...  12.1 us
    reduce_sum x1, other arithmetic, per_device(): jnp.sum(older * image)  9.11 us
    all_to_all x1, starting transfers between devices, sent_and_summed(): lax.all_to_all(parts, axis, split_axis=0, concat_axis=0, tiled=True)  6.78 us
    all_to_all x1, waiting for transfers between devices, from_everyone(): return lax.all_to_all(copies, axis, split_axis=0, concat_axis=0, tiled=True)  6.46 us
  transfers between devices with their start and end apart: 6, of which 5 were waited for; matrix products, arithmetic and copies ran while one was open for 4% of the time, Pallas kernels for 0%

commit v1 on v0

v1 whole, which is shorter than its diff:
```python
import functools

import jax
import jax.numpy as jnp
import ml_dtypes
import numpy as np
from jax import lax
from jax.experimental import pallas as pl
from jax.experimental.pallas import tpu as pltpu
from jax.sharding import PartitionSpec as P

side_weights = (1.5, -0.15, 1.0 / 90.0)
central_weight = -49.0 / 18.0
screening = 1.0 / 64.0
MESH = pl.DeviceIdType.MESH
F32 = jnp.float32
BF16 = jnp.bfloat16


def cas_table(length):
    position = np.arange(length)
    angle = 2.0 * np.pi / length * (position[:, None] * position[None, :] % length)
    return np.cos(angle) + np.sin(angle)


def side_table(length, center):
    table = center * np.eye(length)
    for offset, weight in enumerate(side_weights):
        for shift in (offset + 1, -offset - 1):
            table = table + weight * np.roll(np.eye(length), shift, 0)
    return -0.5 * table


def high_low(table):
    high = table.astype(np.float32).astype(ml_dtypes.bfloat16)
    low = (table - high.astype(np.float64)).astype(np.float32).astype(ml_dtypes.bfloat16)
    return [high, low]


def split(value):
    high = value.astype(BF16)
    return high, (value - high.astype(F32)).astype(BF16)


def dot(a, b):
    return jnp.dot(a, b, preferred_element_type=F32)


def dot3(a, b):
    return dot(a[0], b[0]) + (dot(a[0], b[1]) + dot(a[1], b[0]))


def folded_square(position, length):
    folded = jnp.minimum(position, length - position).astype(F32) * (2.0 * np.pi / length)
    return folded * folded


def partner(me, step, size):
    side = lax.rem(step, 2)
    rank = lax.div(step, 2)
    odd = lax.rem(rank, 2)
    delta = odd * lax.div(rank + 1, 2) - (1 - odd) * lax.div(rank, 2)
    return lax.rem(me + size // 4 + side * (size // 2) + delta, size)


def everyone(me, size, action):
    def one(step, carry):
        action(partner(me, step, size))
        return carry

    lax.fori_loop(0, size - 1, one, 0)


def cyclic(me, size, action):
    def one(step, carry):
        action(lax.rem(me + 1 + step, size))
        return carry

    lax.fori_loop(0, size - 1, one, 0)


def wait_bytes(ref, sem):
    pltpu.make_async_copy(ref, ref, sem).wait()


def kernel(
    nd, no, energies, beta, orb_hbm, loc_hbm, cur_hbm, pre_hbm, t128_hbm, ty_hbm, tx_hbm,
    out_hbm, alpha_out, norm_out,
    orb, loc, cur, pre, t128, ty, tx, out, img, below, above,
    rs_send, rs_recv, a_send, a_recv, b_send, b_recv, g_send, g_recv,
    mo_send, mo_recv, md_send, md_recv, early,
    load_sem, near_sem, send_sem, recv_sem, out_sem,
):
    me = lax.axis_index("dom")
    mine = lax.axis_index("orb")
    count, planes, ny, nz = cur.shape
    rows = ny // no
    half = nz // 2
    barrier = pltpu.get_barrier_semaphore()
    everyone(me, nd, lambda j: pl.semaphore_signal(
        barrier, inc=1, device_id={"dom": j}, device_id_type=MESH))
    cyclic(mine, no, lambda j: pl.semaphore_signal(
        barrier, inc=1, device_id={"orb": j}, device_id_type=MESH))

    loads = [
        pltpu.make_async_copy(s, d, load_sem.at[n])
        for n, (s, d) in enumerate((
            (cur_hbm, cur), (orb_hbm, orb), (t128_hbm, t128), (ty_hbm, ty),
            (pre_hbm, pre), (loc_hbm, loc), (tx_hbm, tx),
        ))
    ]
    for load in loads:
        load.start()
    for load in loads[:4]:
        load.wait()
    cz = (t128[0], t128[1])

    def forward(p, carry):
        field = jnp.zeros((ny, nz), F32)
        for i in range(count):
            field = field + orb[i, p].astype(F32) * cur[i, p].astype(F32)
        field = dot3(split(field), cz)
        field = dot3((ty[0], ty[1]), split(field))
        rs_send[:, p] = field.reshape(no, rows, nz).astype(BF16)
        return carry

    lax.fori_loop(0, planes, forward, 0)
    pl.semaphore_wait(barrier, nd + no - 2)

    cyclic(mine, no, lambda j: pltpu.make_async_remote_copy(
        rs_send.at[j], rs_recv.at[mine], send_sem.at[0], recv_sem.at[0],
        device_id={"orb": j}, device_id_type=MESH).start())
    upward = pltpu.make_async_remote_copy(
        cur.at[:, pl.ds(planes - 3, 3)], below, near_sem.at[0], near_sem.at[1],
        device_id={"dom": lax.rem(me + 1, nd)}, device_id_type=MESH)
    downward = pltpu.make_async_remote_copy(
        cur.at[:, pl.ds(0, 3)], above, near_sem.at[2], near_sem.at[3],
        device_id={"dom": lax.rem(me + nd - 1, nd)}, device_id_type=MESH)
    upward.start()
    downward.start()
    rs_recv[mine] = rs_send[mine]

    for load in loads[4:]:
        load.wait()

    def folded(value):
        return jnp.sum(value.reshape(ny // 8, 8, nz), axis=0)

    def local(n, sums):
        i, p = lax.div(n, planes), lax.rem(n, planes)
        here = cur[i, p]
        value = here.astype(F32)
        old = pre[i, p].astype(F32)
        near = dot(ty[2], here) + dot(ty[3], here)
        near = near + dot(here, t128[2]) + dot(here, t128[3])
        img[i, p] = near + (loc[p] - energies[i]) * value
        return (
            sums[0] + folded(value * value),
            sums[1] + folded(value * old),
            sums[2] + folded(old * old),
        )

    zero = jnp.zeros((8, nz), F32)
    known = lax.fori_loop(0, count * planes, local, (zero, zero, zero))
    for n in range(3):
        early[n] = known[n]

    lane = lax.broadcasted_iota(jnp.int32, (rows, nz), 1)
    low = lane < half

    wait_bytes(rs_recv.at[pl.ds(0, no - 1)], recv_sem.at[0])
    s = []
    for p in range(planes):
        total = rs_recv[0, p].astype(F32)
        for o in range(1, no):
            total = total + rs_recv[o, p].astype(F32)
        s.append(total)
    turned = [pltpu.roll(v, half, 1) for v in s]
    for q in range(2):
        a_send[:rows, q, :] = jnp.where(low, s[q], turned[q + 2])
        a_send[rows:, q, :] = jnp.where(low, turned[q], s[q + 2])

    def slot(j):
        return lax.rem(j, 2) * rows + lax.div(j, 2)

    def all_to_all(source, target, n):
        everyone(me, nd, lambda j: pltpu.make_async_remote_copy(
            source.at[slot(j)], target.at[slot(me)], send_sem.at[n], recv_sem.at[n],
            device_id={"dom": j}, device_id_type=MESH).start())
        target[slot(me)] = source[slot(me)]

    all_to_all(a_send, a_recv, 1)

    upward.wait()
    downward.wait()

    def lines(i, carry):
        line = [below[i, p].astype(F32) for p in range(3)]
        line = line + [cur[i, p].astype(F32) for p in range(planes)]
        line = line + [above[i, p].astype(F32) for p in range(3)]
        for p in range(planes):
            value = img[i, p]
            for n, weight in enumerate(side_weights):
                value = value + (-0.5 * weight) * (line[p + 4 + n] + line[p + 2 - n])
            img[i, p] = value
        return carry

    lax.fori_loop(0, count, lines, 0)

    row = mine * rows + lax.div(me, 2)
    column = lax.rem(me, 2) * half + lax.rem(
        lax.broadcasted_iota(jnp.int32, (1, nz), 1), half)
    nx = nd * planes
    kx = folded_square(lax.broadcasted_iota(jnp.int32, (nx, nz), 0), nx)
    ky = folded_square(jnp.full((1, nz), row, jnp.int32), ny)
    weight = (4.0 * np.pi / (nx * ny * nz)) / (kx + (ky + folded_square(column, nz) + screening))
    wide = lax.broadcasted_iota(jnp.int32, (nx, nz), 1) < half

    wait_bytes(a_recv.at[pl.ds(0, nd - 1)], recv_sem.at[1])
    gathered = split(jnp.concatenate([a_recv[:, q, :] for q in range(2)], axis=0))
    size = nx // 2
    first = dot3((tx[0, :, :size], tx[1, :, :size]), gathered)
    second = dot3((tx[0, :, size:], tx[1, :, size:]), gathered)
    modes = jnp.where(
        wide, first + pltpu.roll(second, half, 1), pltpu.roll(first, half, 1) + second)
    modes = split(modes * weight)
    back = dot3((tx[2], tx[3]), modes)
    back = jnp.where(wide[:size], back[:size], back[size:])
    for q in range(2):
        b_send[:, q, :] = back[q * nd : (q + 1) * nd]

    all_to_all(b_send, b_recv, 2)
    wait_bytes(b_recv.at[pl.ds(0, nd - 1)], recv_sem.at[2])
    for q in range(2):
        even, odd = b_recv[:rows, q, :], b_recv[rows:, q, :]
        g_send[q] = jnp.where(low, even, pltpu.roll(odd, half, 1)).astype(BF16)
        g_send[q + 2] = jnp.where(low, pltpu.roll(even, half, 1), odd).astype(BF16)

    cyclic(mine, no, lambda j: pltpu.make_async_remote_copy(
        g_send, g_recv.at[mine], send_sem.at[3], recv_sem.at[3],
        device_id={"orb": j}, device_id_type=MESH).start())
    g_recv[mine] = g_send[...]
    wait_bytes(g_recv.at[pl.ds(0, no - 1)], recv_sem.at[3])

    def finish(p, sums):
        field = g_recv[:, p].reshape(ny, nz)
        field = dot(ty[0], field) + dot(ty[1], field)
        field = dot3(split(field), cz)
        for i in range(count):
            value = img[i, p] + orb[i, p].astype(F32) * field
            img[i, p] = value
            sums = (
                sums[0] + folded(cur[i, p].astype(F32) * value),
                sums[1] + folded(value * value),
                sums[2] + folded(pre[i, p].astype(F32) * value),
            )
        return sums

    late = lax.fori_loop(0, planes, finish, (zero, zero, zero))
    ones = lax.broadcasted_iota(jnp.int32, (1, nz), 1)

    def whole(value):
        return jnp.sum(jnp.sum(value, axis=0, keepdims=True), axis=1, keepdims=True)

    packed = jnp.zeros((1, nz), F32)
    for n, value in enumerate((*late, early[0], early[1], early[2])):
        packed = jnp.where(ones == n, whole(value), packed)
    mo_send[...] = packed
    cyclic(mine, no, lambda j: pltpu.make_async_remote_copy(
        mo_send, mo_recv.at[mine], send_sem.at[4], recv_sem.at[4],
        device_id={"orb": j}, device_id_type=MESH).start())
    mo_recv[mine] = packed
    wait_bytes(mo_recv.at[pl.ds(0, no - 1)], recv_sem.at[4])
    packed = jnp.sum(mo_recv[...], axis=0)
    md_send[...] = packed
    everyone(me, nd, lambda j: pltpu.make_async_remote_copy(
        md_send, md_recv.at[me], send_sem.at[5], recv_sem.at[5],
        device_id={"dom": j}, device_id_type=MESH).start())
    md_recv[me] = packed
    wait_bytes(md_recv.at[pl.ds(0, nd - 1)], recv_sem.at[5])
    packed = jnp.sum(md_recv[...], axis=0) * (1.0 / (count * no * nx * ny * nz))

    cross, image, older_image, own, mixed, older = [
        jnp.sum(jnp.where(ones == n, packed, 0.0), axis=1, keepdims=True) for n in range(6)
    ]
    beta_now = beta[0]
    squares = image - 2.0 * cross * cross - 2.0 * beta_now * older_image
    squares = squares + cross * cross * own + 2.0 * cross * beta_now * mixed
    squares = squares + beta_now * beta_now * older
    norm = jnp.sqrt(squares + 1e-06)
    inverse = 1.0 / norm
    alpha_out[0] = cross[0, 0]
    norm_out[0] = norm[0, 0]

    def scale(n, carry):
        i, p = lax.div(n, planes), lax.rem(n, planes)
        value = img[i, p] - cross * cur[i, p].astype(F32) - beta_now * pre[i, p].astype(F32)
        out[i, p] = (value * inverse).astype(BF16)
        return carry

    lax.fori_loop(0, count * planes, scale, 0)
    store = pltpu.make_async_copy(out, out_hbm, out_sem)
    store.start()
    wait_bytes(rs_send.at[pl.ds(0, no - 1)], send_sem.at[0])
    wait_bytes(a_send.at[pl.ds(0, nd - 1)], send_sem.at[1])
    wait_bytes(b_send.at[pl.ds(0, nd - 1)], send_sem.at[2])
    wait_bytes(g_recv.at[pl.ds(0, no - 1)], send_sem.at[3])
    wait_bytes(mo_recv.at[pl.ds(0, no - 1)], send_sem.at[4])
    wait_bytes(md_recv.at[pl.ds(0, nd - 1)], send_sem.at[5])
    store.wait()


def per_device(nd, no, orbitals, energies, local_potential, lanczos, previous, beta):
    count, planes, ny, nz = lanczos.shape
    rows, nx = ny // no, nd * planes
    order = np.array([
        planes * (2 * r + h) + 2 * lane_half + q
        for lane_half in range(2) for q in range(2) for h in range(2) for r in range(rows)
    ])
    cas_x = cas_table(nx)
    t128 = np.stack(high_low(cas_table(nz)) + high_low(side_table(nz, central_weight)))
    ty = np.stack(high_low(cas_table(ny)) + high_low(side_table(ny, 2.0 * central_weight)))
    tx = np.stack(high_low(cas_x[:, order]) + high_low(cas_x[order, :]))
    hbm = pl.BlockSpec(memory_space=pl.ANY)
    smem = pl.BlockSpec(memory_space=pltpu.SMEM)
    vmem = pltpu.VMEM
    field = (count, planes, ny, nz)
    dma = pltpu.SemaphoreType.DMA
    return pl.pallas_call(
        functools.partial(kernel, nd, no),
        out_shape=(
            jax.ShapeDtypeStruct(field, BF16),
            jax.ShapeDtypeStruct((1,), F32),
            jax.ShapeDtypeStruct((1,), F32),
        ),
        in_specs=[smem, smem] + [hbm] * 7,
        out_specs=(hbm, smem, smem),
        scratch_shapes=[
            vmem(field, BF16), vmem(field[1:], F32), vmem(field, BF16), vmem(field, BF16),
            vmem(t128.shape, BF16), vmem(ty.shape, BF16), vmem(tx.shape, BF16),
            vmem(field, BF16), vmem(field, F32),
            vmem((count, 3, ny, nz), BF16), vmem((count, 3, ny, nz), BF16),
            vmem((no, planes, rows, nz), BF16), vmem((no, planes, rows, nz), BF16),
            vmem((nd, 2, nz), F32), vmem((nd, 2, nz), F32),
            vmem((nd, 2, nz), F32), vmem((nd, 2, nz), F32),
            vmem((planes, rows, nz), BF16), vmem((no, planes, rows, nz), BF16),
            vmem((1, nz), F32), vmem((no, 1, nz), F32),
            vmem((1, nz), F32), vmem((nd, 1, nz), F32),
            vmem((3, 8, nz), F32),
            dma((7,)), dma((4,)), dma((6,)), dma((6,)), dma(()),
        ],
        compiler_params=pltpu.CompilerParams(collective_id=0, has_side_effects=True),
    )(energies, beta, orbitals, local_potential, lanczos, previous,
      jnp.asarray(t128), jnp.asarray(ty), jnp.asarray(tx))


def solution(mesh):
    placed = (
        P("orb", "dom", None, None),
        P("orb"),
        P("dom", None, None),
        P("orb", "dom", None, None),
        P("orb", "dom", None, None),
        P(),
    )
    return jax.shard_map(
        functools.partial(per_device, mesh.shape["dom"], mesh.shape["orb"]),
        mesh=mesh,
        in_specs=placed,
        out_specs=(P("orb", "dom", None, None), P(), P()),
        check_vma=False,
    )
```

time: 206 us -> 71.8 us (0.35); the launches traced: 203 us -> 71.6 us
  Pallas kernels: 0 us -> 65 us
  blocking collectives: 51.1 us -> 0 us
  starting transfers between devices: 44.4 us -> 0 us
  waiting for transfers between devices: 39.6 us -> 0 us
  local copies, waits for them, and re-layouts: 28.4 us -> 1.87 us
  other arithmetic: 19.5 us -> 0 us
  matrix products: 10.2 us -> 0 us
  between operations: 9.51 us -> 4.75 us
    pallas_call x0 -> x1, Pallas kernels: none -> 65 us  [per_device(): pl.pallas_call(functools.partial(kernel, nd, no), out_shape=(jax.ShapeDty...]
    psum x5 -> x0, blocking collectives: 51.1 us -> none  [over_axes(): array = lax.psum(array, axis)]
    all_to_all x4 -> x0, waiting for transfers between devices: 36.7 us -> none  [the longest x1 12.8 us: per_device(): lax.all_to_all(flattened, DOM, split_axis=1, concat_axis=0, tiled=True)]
    all_to_all x4 -> x0, starting transfers between devices: 33.7 us -> none  [the longest x1 18.2 us: per_device(): lax.all_to_all(flattened, DOM, split_axis=1, concat_axis=0, tiled=True)]
    slice x10 -> x0, local copies, waits for them, and re-layouts: 15.7 us -> none  [the longest x9 14.5 us: per_device(): jnp.roll(current, reach, dimension) + jnp.roll(current, -reach, dimension)]
    reduce_sum x3 -> x0, other arithmetic: 11.8 us -> none  [the longest x1 9.11 us: per_device(): jnp.sum(older * image)]
    ppermute x2 -> x0, starting transfers between devices: 10.7 us -> none  [the longest x1 5.74 us: extended(): after = lax.ppermute(first, axis, down)]
    dot_general x6 -> x0, matrix products: 10.2 us -> none  [the longest x2 3.38 us: transform_lateral(): jnp.einsum('by,ayz->abz', cas_table(values.shape[1]), values, precision=h...]
  transfers between devices with their start and end apart: 6 -> 0, of which waited for: 5 -> 0; matrix products, arithmetic and copies ran while one was open for 4% -> 0% of each run, Pallas kernels for 0% -> 0%
where the time goes in v1:
time: 71.8 us; the launch traced here: 71.6 us
  Pallas kernels  65 us (91%)
  between operations  4.75 us (7%)
  local copies, waits for them, and re-layouts  1.87 us (3%)
    pallas_call x1, Pallas kernels, per_device(): pl.pallas_call(functools.partial(kernel, nd, no), out_shape=(jax.ShapeDty...  65 us
    unnamed x1, local copies, waits for them, and re-layouts  1.87 us

profile of v1, /device:TPU:1, one launch (start us, length us, event | category | flops | bytes accessed | tf_op | source)
XLA Modules:
  0.0 71.6 jit_solution(29384413985894744)
XLA Ops:
  1.3 65.0 %shard_map.112 = (bf16[2,4,256,128]{3,2,1,0:T(8,128)(2,1)}, f32[1]{0:T(128)}, f32[1]{0:T(128)}) custom-call(f32[2]{0:T(128)} %energies.1, f32[1]{0:T(128)S(6)} %copy.15.beta, bf16[2,4,256,128]{3,2,1,0:T(8,128)(2,1)} %orb_hbm.1, f32[4,256,128]{2,1,0:T(8,128)} %loc_hbm.1, bf16[2,4,256,128]{3,2,1,0:T(8,128)(2,1)} %cur_hbm.1, bf16[2,4,256,128]{3,2,1,0:T(8,128)(2,1)} %pre_hbm.1, ...), custom_call_target="tpu_custom_call" | custom-call | tf_op jit(solution)/shard_map/pallas_call | solution.py:329
  66.3 1.9 %copy.16 = bf16[2,4,256,128]{3,2,1,0:T(8,128)(2,1)} copy(bf16[2,4,256,128]{3,2,1,0:T(8,128)(2,1)} %get-tuple-element.6) | data formatting | bytes 1048576

commit v2 on v1

--- a/solution.py
+++ b/solution.py
@@ -55,28 +55,26 @@
     return folded * folded
 
 
-def partner(me, step, size):
-    side = lax.rem(step, 2)
-    rank = lax.div(step, 2)
-    odd = lax.rem(rank, 2)
-    delta = odd * lax.div(rank + 1, 2) - (1 - odd) * lax.div(rank, 2)
-    return lax.rem(me + size // 4 + side * (size // 2) + delta, size)
-
-
 def everyone(me, size, action):
-    def one(step, carry):
-        action(partner(me, step, size))
+    quarter = size // 4
+    around = lambda offset: action(lax.rem(me + offset, size))
+    around(quarter)
+    around(3 * quarter)
+
+    def nearer(step, carry):
+        around(quarter + step)
+        around(quarter - step)
+        around(3 * quarter + step)
+        around(3 * quarter - step)
         return carry
 
-    lax.fori_loop(0, size - 1, one, 0)
+    lax.fori_loop(1, quarter, nearer, 0)
+    around(2 * quarter)
 
 
 def cyclic(me, size, action):
-    def one(step, carry):
-        action(lax.rem(me + 1 + step, size))
-        return carry
-
-    lax.fori_loop(0, size - 1, one, 0)
+    for step in range(1, size):
+        action(lax.rem(me + step, size))
 
 
 def wait_bytes(ref, sem):
@@ -84,33 +82,34 @@
 
 
 def kernel(
-    nd, no, energies, beta, orb_hbm, loc_hbm, cur_hbm, pre_hbm, t128_hbm, ty_hbm, tx_hbm,
-    out_hbm, alpha_out, norm_out,
-    orb, loc, cur, pre, t128, ty, tx, out, img, below, above,
+    nd, no, energies_hbm, beta_hbm, orb_hbm, loc_hbm, cur_hbm, pre_hbm, t128_hbm, ty_hbm, tx_hbm,
+    out, alpha_out, norm_out,
+    orb, loc, cur, pre, t128, ty, tx, img, below, above,
     rs_send, rs_recv, a_send, a_recv, b_send, b_recv, g_send, g_recv,
-    mo_send, mo_recv, md_send, md_recv, early,
-    load_sem, near_sem, send_sem, recv_sem, out_sem,
+    mo_send, mo_recv, md_send, md_recv, early, stage, energies, beta,
+    load_sem, near_sem, send_sem, recv_sem, plane_sem,
 ):
     me = lax.axis_index("dom")
     mine = lax.axis_index("orb")
     count, planes, ny, nz = cur.shape
     rows = ny // no
     half = nz // 2
+    loads = [
+        pltpu.make_async_copy(s, d, load_sem.at[n])
+        for n, (s, d) in enumerate((
+            (cur_hbm, cur), (orb_hbm, orb), (t128_hbm, t128), (ty_hbm, ty),
+            (pre_hbm, pre), (loc_hbm, loc), (tx_hbm, tx),
+            (energies_hbm, energies), (beta_hbm, beta),
+        ))
+    ]
+    for load in loads:
+        load.start()
     barrier = pltpu.get_barrier_semaphore()
     everyone(me, nd, lambda j: pl.semaphore_signal(
         barrier, inc=1, device_id={"dom": j}, device_id_type=MESH))
     cyclic(mine, no, lambda j: pl.semaphore_signal(
         barrier, inc=1, device_id={"orb": j}, device_id_type=MESH))
 
-    loads = [
-        pltpu.make_async_copy(s, d, load_sem.at[n])
-        for n, (s, d) in enumerate((
-            (cur_hbm, cur), (orb_hbm, orb), (t128_hbm, t128), (ty_hbm, ty),
-            (pre_hbm, pre), (loc_hbm, loc), (tx_hbm, tx),
-        ))
-    ]
-    for load in loads:
-        load.start()
     for load in loads[:4]:
         load.wait()
     cz = (t128[0], t128[1])
@@ -136,8 +135,18 @@
     downward = pltpu.make_async_remote_copy(
         cur.at[:, pl.ds(0, 3)], above, near_sem.at[2], near_sem.at[3],
         device_id={"dom": lax.rem(me + nd - 1, nd)}, device_id_type=MESH)
-    upward.start()
-    downward.start()
+    turn = nd // 2
+    top = lax.rem(me, turn) == turn - 1
+    bottom = lax.rem(me, turn) == 0
+
+    @pl.when(jnp.logical_not(top))
+    def _():
+        upward.start()
+
+    @pl.when(jnp.logical_not(bottom))
+    def _():
+        downward.start()
+
     rs_recv[mine] = rs_send[mine]
 
     for load in loads[4:]:
@@ -177,8 +186,9 @@
         s.append(total)
     turned = [pltpu.roll(v, half, 1) for v in s]
     for q in range(2):
-        a_send[:rows, q, :] = jnp.where(low, s[q], turned[q + 2])
-        a_send[rows:, q, :] = jnp.where(low, turned[q], s[q + 2])
+        stage[:rows, q, :] = jnp.where(low, s[q], turned[q + 2])
+        stage[rows:, q, :] = jnp.where(low, turned[q], s[q + 2])
+    a_send[...] = stage[...].astype(BF16)
 
     def slot(j):
         return lax.rem(j, 2) * rows + lax.div(j, 2)
@@ -191,6 +201,39 @@
 
     all_to_all(a_send, a_recv, 1)
 
+    @pl.when(top)
+    def _():
+        upward.start()
+
+    @pl.when(bottom)
+    def _():
+        downward.start()
+
+    row = mine * rows + lax.div(me, 2)
+    column = lax.rem(me, 2) * half + lax.rem(
+        lax.broadcasted_iota(jnp.int32, (1, nz), 1), half)
+    nx = nd * planes
+    kx = folded_square(lax.broadcasted_iota(jnp.int32, (nx, nz), 0), nx)
+    ky = folded_square(jnp.full((1, nz), row, jnp.int32), ny)
+    weight = (4.0 * np.pi / (nx * ny * nz)) / (kx + (ky + folded_square(column, nz) + screening))
+    wide = lax.broadcasted_iota(jnp.int32, (nx, nz), 1) < half
+
+    wait_bytes(a_recv.at[pl.ds(0, nd - 1)], recv_sem.at[1])
+    stage[...] = a_recv[...].astype(F32)
+    gathered = jnp.concatenate([stage[:, q, :] for q in range(2)], axis=0).astype(BF16)
+    size = nx // 2
+    first = dot(tx[0, :, :size], gathered) + dot(tx[1, :, :size], gathered)
+    second = dot(tx[0, :, size:], gathered) + dot(tx[1, :, size:], gathered)
+    modes = jnp.where(
+        wide, first + pltpu.roll(second, half, 1), pltpu.roll(first, half, 1) + second)
+    modes = split(modes * weight)
+    back = dot3((tx[2], tx[3]), modes)
+    back = jnp.where(wide[:size], back[:size], back[size:])
+    for q in range(2):
+        stage[:, q, :] = back[q * nd : (q + 1) * nd]
+    b_send[...] = stage[...].astype(BF16)
+
+    all_to_all(b_send, b_recv, 2)
     upward.wait()
     downward.wait()
 
@@ -207,42 +250,21 @@
 
     lax.fori_loop(0, count, lines, 0)
 
-    row = mine * rows + lax.div(me, 2)
-    column = lax.rem(me, 2) * half + lax.rem(
-        lax.broadcasted_iota(jnp.int32, (1, nz), 1), half)
-    nx = nd * planes
-    kx = folded_square(lax.broadcasted_iota(jnp.int32, (nx, nz), 0), nx)
-    ky = folded_square(jnp.full((1, nz), row, jnp.int32), ny)
-    weight = (4.0 * np.pi / (nx * ny * nz)) / (kx + (ky + folded_square(column, nz) + screening))
-    wide = lax.broadcasted_iota(jnp.int32, (nx, nz), 1) < half
-
-    wait_bytes(a_recv.at[pl.ds(0, nd - 1)], recv_sem.at[1])
-    gathered = split(jnp.concatenate([a_recv[:, q, :] for q in range(2)], axis=0))
-    size = nx // 2
-    first = dot3((tx[0, :, :size], tx[1, :, :size]), gathered)
-    second = dot3((tx[0, :, size:], tx[1, :, size:]), gathered)
-    modes = jnp.where(
-        wide, first + pltpu.roll(second, half, 1), pltpu.roll(first, half, 1) + second)
-    modes = split(modes * weight)
-    back = dot3((tx[2], tx[3]), modes)
-    back = jnp.where(wide[:size], back[:size], back[size:])
+    wait_bytes(b_recv.at[pl.ds(0, nd - 1)], recv_sem.at[2])
+    stage[...] = b_recv[...].astype(F32)
     for q in range(2):
-        b_send[:, q, :] = back[q * nd : (q + 1) * nd]
-
-    all_to_all(b_send, b_recv, 2)
-    wait_bytes(b_recv.at[pl.ds(0, nd - 1)], recv_sem.at[2])
-    for q in range(2):
-        even, odd = b_recv[:rows, q, :], b_recv[rows:, q, :]
+        even, odd = stage[:rows, q, :], stage[rows:, q, :]
         g_send[q] = jnp.where(low, even, pltpu.roll(odd, half, 1)).astype(BF16)
         g_send[q + 2] = jnp.where(low, pltpu.roll(even, half, 1), odd).astype(BF16)
 
-    cyclic(mine, no, lambda j: pltpu.make_async_remote_copy(
-        g_send, g_recv.at[mine], send_sem.at[3], recv_sem.at[3],
-        device_id={"orb": j}, device_id_type=MESH).start())
+    for p in range(planes):
+        cyclic(mine, no, lambda j: pltpu.make_async_remote_copy(
+            g_send.at[p], g_recv.at[mine, p], send_sem.at[3], plane_sem.at[p],
+            device_id={"orb": j}, device_id_type=MESH).start())
     g_recv[mine] = g_send[...]
-    wait_bytes(g_recv.at[pl.ds(0, no - 1)], recv_sem.at[3])
 
     def finish(p, sums):
+        wait_bytes(g_recv.at[pl.ds(0, no - 1), p], plane_sem.at[p])
         field = g_recv[:, p].reshape(ny, nz)
         field = dot(ty[0], field) + dot(ty[1], field)
         field = dot3(split(field), cz)
@@ -299,15 +321,12 @@
         return carry
 
     lax.fori_loop(0, count * planes, scale, 0)
-    store = pltpu.make_async_copy(out, out_hbm, out_sem)
-    store.start()
     wait_bytes(rs_send.at[pl.ds(0, no - 1)], send_sem.at[0])
     wait_bytes(a_send.at[pl.ds(0, nd - 1)], send_sem.at[1])
     wait_bytes(b_send.at[pl.ds(0, nd - 1)], send_sem.at[2])
     wait_bytes(g_recv.at[pl.ds(0, no - 1)], send_sem.at[3])
     wait_bytes(mo_recv.at[pl.ds(0, no - 1)], send_sem.at[4])
     wait_bytes(md_recv.at[pl.ds(0, nd - 1)], send_sem.at[5])
-    store.wait()
 
 
 def per_device(nd, no, orbitals, energies, local_potential, lanczos, previous, beta):
@@ -329,25 +348,26 @@
     return pl.pallas_call(
         functools.partial(kernel, nd, no),
         out_shape=(
-            jax.ShapeDtypeStruct(field, BF16),
+            pltpu.VMEM(field, BF16),
             jax.ShapeDtypeStruct((1,), F32),
             jax.ShapeDtypeStruct((1,), F32),
         ),
-        in_specs=[smem, smem] + [hbm] * 7,
-        out_specs=(hbm, smem, smem),
+        in_specs=[hbm] * 9,
+        out_specs=(pl.BlockSpec(memory_space=vmem), smem, smem),
         scratch_shapes=[
             vmem(field, BF16), vmem(field[1:], F32), vmem(field, BF16), vmem(field, BF16),
             vmem(t128.shape, BF16), vmem(ty.shape, BF16), vmem(tx.shape, BF16),
-            vmem(field, BF16), vmem(field, F32),
+            vmem(field, F32),
             vmem((count, 3, ny, nz), BF16), vmem((count, 3, ny, nz), BF16),
             vmem((no, planes, rows, nz), BF16), vmem((no, planes, rows, nz), BF16),
-            vmem((nd, 2, nz), F32), vmem((nd, 2, nz), F32),
-            vmem((nd, 2, nz), F32), vmem((nd, 2, nz), F32),
+            vmem((nd, 2, nz), BF16), vmem((nd, 2, nz), BF16),
+            vmem((nd, 2, nz), BF16), vmem((nd, 2, nz), BF16),
             vmem((planes, rows, nz), BF16), vmem((no, planes, rows, nz), BF16),
             vmem((1, nz), F32), vmem((no, 1, nz), F32),
             vmem((1, nz), F32), vmem((nd, 1, nz), F32),
-            vmem((3, 8, nz), F32),
-            dma((7,)), dma((4,)), dma((6,)), dma((6,)), dma(()),
+            vmem((3, 8, nz), F32), vmem((nd, 2, nz), F32),
+            pltpu.SMEM((count,), F32), pltpu.SMEM((1,), F32),
+            dma((9,)), dma((4,)), dma((6,)), dma((6,)), dma((planes,)),
         ],
         compiler_params=pltpu.CompilerParams(collective_id=0, has_side_effects=True),
     )(energies, beta, orbitals, local_potential, lanczos, previous,

time: 71.8 us -> 64.5 us (0.90)
  Pallas kernels: 65 us -> 58.7 us
  local copies, waits for them, and re-layouts: 1.87 us -> 0.8 us
    pallas_call x1, Pallas kernels: 65 us -> 58.7 us  [per_device(): pl.pallas_call(functools.partial(kernel, nd, no), out_shape=(pltpu.VMEM(f...]
    unnamed x1, local copies, waits for them, and re-layouts: 1.87 us -> 0.8 us
where the time goes in v2:
time: 64.5 us; the launch traced here: 64.3 us
  Pallas kernels  58.7 us (91%)
  between operations  4.74 us (7%)
  local copies, waits for them, and re-layouts  0.8 us (1%)
    pallas_call x1, Pallas kernels, per_device(): pl.pallas_call(functools.partial(kernel, nd, no), out_shape=(pltpu.VMEM(f...  58.7 us

profile of v2, /device:TPU:1, one launch (start us, length us, event | category | flops | bytes accessed | tf_op | source)
XLA Modules:
  0.0 64.3 jit_solution(4215559640679760433)
XLA Ops:
  1.3 58.7 %shard_map.112 = (bf16[2,4,256,128]{3,2,1,0:T(8,128)(2,1)S(1)}, f32[1]{0:T(128)}, f32[1]{0:T(128)}) custom-call(f32[2]{0:T(128)} %energies_hbm.1, f32[1]{0:T(128)S(6)} %copy.16.beta_hbm, bf16[2,4,256,128]{3,2,1,0:T(8,128)(2,1)} %orb_hbm.1, f32[4,256,128]{2,1,0:T(8,128)} %loc_hbm.1, bf16[2,4,256,128]{3,2,1,0:T(8,128)(2,1)} %cur_hbm.1, ...), custom_call_target="tpu_custom_call" | custom-call | tf_op jit(solution)/shard_map/pallas_call | solution.py:348
  60.0 0.8 %copy.15 = bf16[2,4,256,128]{3,2,1,0:T(8,128)(2,1)} copy(bf16[2,4,256,128]{3,2,1,0:T(8,128)(2,1)S(1)} %get-tuple-element.3) | data formatting | bytes 1048576

commit v3 on v2

--- a/solution.py
+++ b/solution.py
@@ -86,8 +86,8 @@
     out, alpha_out, norm_out,
     orb, loc, cur, pre, t128, ty, tx, img, below, above,
     rs_send, rs_recv, a_send, a_recv, b_send, b_recv, g_send, g_recv,
-    mo_send, mo_recv, md_send, md_recv, early, stage, energies, beta,
-    load_sem, near_sem, send_sem, recv_sem, plane_sem,
+    mo_send, mo_recv, md_send, md_recv, early, stage, mixed_fields, potential, energies, beta,
+    load_sem, near_sem, send_sem, recv_sem, plane_sem, heard, all_heard,
 ):
     me = lax.axis_index("dom")
     mine = lax.axis_index("orb")
@@ -104,11 +104,28 @@
     ]
     for load in loads:
         load.start()
+    ring = nd // 4
+    core = lax.rem(me, 2)
+    wide_x = lax.div(me, nd // 2)
+    depth = lax.rem(lax.div(me, 2), ring)
+
+    def along(offset):
+        return wide_x * (nd // 2) + lax.rem(depth + offset + ring, ring) * 2 + core
+
+    def beside(a, b):
+        return lax.rem(wide_x + a, 2) * (nd // 2) + depth * 2 + lax.rem(core + b, 2)
+
+    outer = lax.rem(me + 2 * core - 1 + nd, nd)
+    chips = ((1, 1), (1, 0), (0, 1))
+
+    def tell(sem, j):
+        pl.semaphore_signal(sem, inc=1, device_id={"dom": j}, device_id_type=MESH)
+
     barrier = pltpu.get_barrier_semaphore()
-    everyone(me, nd, lambda j: pl.semaphore_signal(
-        barrier, inc=1, device_id={"dom": j}, device_id_type=MESH))
     cyclic(mine, no, lambda j: pl.semaphore_signal(
         barrier, inc=1, device_id={"orb": j}, device_id_type=MESH))
+    for j in [beside(*c) for c in chips] + [along(1), along(-1), outer]:
+        tell(barrier, j)
 
     for load in loads[:4]:
         load.wait()
@@ -123,12 +140,27 @@
         rs_send[:, p] = field.reshape(no, rows, nz).astype(BF16)
         return carry
 
-    lax.fori_loop(0, planes, forward, 0)
-    pl.semaphore_wait(barrier, nd + no - 2)
-
-    cyclic(mine, no, lambda j: pltpu.make_async_remote_copy(
-        rs_send.at[j], rs_recv.at[mine], send_sem.at[0], recv_sem.at[0],
-        device_id={"orb": j}, device_id_type=MESH).start())
+    def spread(n, stride):
+        tell(heard.at[n], along(stride))
+        tell(heard.at[n], along(-stride))
+
+    strides = [1]
+    while 2 * sum(strides, 1) < ring:
+        strides.append(sum(strides, 1))
+    def scatter(p):
+        cyclic(mine, no, lambda j: pltpu.make_async_remote_copy(
+            rs_send.at[j, p], rs_recv.at[mine, p], send_sem.at[0], recv_sem.at[0],
+            device_id={"orb": j}, device_id_type=MESH).start())
+
+    first = planes // 2
+    lax.fori_loop(0, first, forward, 0)
+    pl.semaphore_wait(barrier, no + 5)
+    spread(0, strides[0])
+    for p in range(first):
+        scatter(p)
+    for p in range(first, planes):
+        forward(p, 0)
+        scatter(p)
     upward = pltpu.make_async_remote_copy(
         cur.at[:, pl.ds(planes - 3, 3)], below, near_sem.at[0], near_sem.at[1],
         device_id={"dom": lax.rem(me + 1, nd)}, device_id_type=MESH)
@@ -170,7 +202,16 @@
         )
 
     zero = jnp.zeros((8, nz), F32)
-    known = lax.fori_loop(0, count * planes, local, (zero, zero, zero))
+    known = (zero, zero, zero)
+    piece = count * planes // len(strides)
+    for n in range(len(strides)):
+        stop = count * planes if n == len(strides) - 1 else (n + 1) * piece
+        known = lax.fori_loop(n * piece, stop, local, known)
+        pl.semaphore_wait(heard.at[n], 2)
+        if n + 1 < len(strides):
+            spread(n + 1, strides[n + 1])
+    for c in chips:
+        tell(all_heard, beside(*c))
     for n in range(3):
         early[n] = known[n]
 
@@ -199,6 +240,7 @@
             device_id={"dom": j}, device_id_type=MESH).start())
         target[slot(me)] = source[slot(me)]
 
+    pl.semaphore_wait(all_heard, 3)
     all_to_all(a_send, a_recv, 1)
 
     @pl.when(top)
@@ -250,6 +292,29 @@
 
     lax.fori_loop(0, count, lines, 0)
 
+    def prepare(p, sums):
+        pair = jnp.zeros((ny, nz), F32)
+        aged, based, square = pair, pair, pair
+        for i in range(count):
+            base, weight_o = img[i, p], orb[i, p].astype(F32)
+            value, old = cur[i, p].astype(F32), pre[i, p].astype(F32)
+            pair = pair + weight_o * value
+            aged = aged + weight_o * old
+            based = based + weight_o * base
+            square = square + weight_o * weight_o
+            sums = (
+                sums[0] + folded(value * base),
+                sums[1] + folded(base * base),
+                sums[2] + folded(old * base),
+            )
+        for n, field in enumerate((pair, aged, 2.0 * based, square)):
+            mixed_fields[n, p] = field
+        return sums
+
+    based = lax.fori_loop(0, planes, prepare, (zero, zero, zero))
+    for n in range(3):
+        early[3 + n] = based[n]
+
     wait_bytes(b_recv.at[pl.ds(0, nd - 1)], recv_sem.at[2])
     stage[...] = b_recv[...].astype(F32)
     for q in range(2):
@@ -268,17 +333,14 @@
         field = g_recv[:, p].reshape(ny, nz)
         field = dot(ty[0], field) + dot(ty[1], field)
         field = dot3(split(field), cz)
-        for i in range(count):
-            value = img[i, p] + orb[i, p].astype(F32) * field
-            img[i, p] = value
-            sums = (
-                sums[0] + folded(cur[i, p].astype(F32) * value),
-                sums[1] + folded(value * value),
-                sums[2] + folded(pre[i, p].astype(F32) * value),
-            )
-        return sums
-
-    late = lax.fori_loop(0, planes, finish, (zero, zero, zero))
+        potential[p] = field
+        return (
+            sums[0] + folded(mixed_fields[0, p] * field),
+            sums[1] + folded((mixed_fields[2, p] + mixed_fields[3, p] * field) * field),
+            sums[2] + folded(mixed_fields[1, p] * field),
+        )
+
+    late = lax.fori_loop(0, planes, finish, (early[3], early[4], early[5]))
     ones = lax.broadcasted_iota(jnp.int32, (1, nz), 1)
 
     def whole(value):
@@ -288,18 +350,24 @@
     for n, value in enumerate((*late, early[0], early[1], early[2])):
         packed = jnp.where(ones == n, whole(value), packed)
     mo_send[...] = packed
-    cyclic(mine, no, lambda j: pltpu.make_async_remote_copy(
-        mo_send, mo_recv.at[mine], send_sem.at[4], recv_sem.at[4],
-        device_id={"orb": j}, device_id_type=MESH).start())
-    mo_recv[mine] = packed
-    wait_bytes(mo_recv.at[pl.ds(0, no - 1)], recv_sem.at[4])
+    here = mine * 4 + wide_x * 2 + core
+    for step in range(no):
+        for c in chips + ((0, 0),):
+            if step or c != (0, 0):
+                pltpu.make_async_remote_copy(
+                    mo_send, mo_recv.at[here], send_sem.at[4], recv_sem.at[4],
+                    device_id={"dom": beside(*c), "orb": lax.rem(mine + step, no)},
+                    device_id_type=MESH).start()
+    mo_recv[here] = packed
+    wait_bytes(mo_recv.at[pl.ds(0, 4 * no - 1)], recv_sem.at[4])
     packed = jnp.sum(mo_recv[...], axis=0)
     md_send[...] = packed
-    everyone(me, nd, lambda j: pltpu.make_async_remote_copy(
-        md_send, md_recv.at[me], send_sem.at[5], recv_sem.at[5],
-        device_id={"dom": j}, device_id_type=MESH).start())
-    md_recv[me] = packed
-    wait_bytes(md_recv.at[pl.ds(0, nd - 1)], recv_sem.at[5])
+    for step in sorted(range(1, ring), key=lambda n: abs(2 * n - ring)):
+        pltpu.make_async_remote_copy(
+            md_send, md_recv.at[depth], send_sem.at[5], recv_sem.at[5],
+            device_id={"dom": along(step)}, device_id_type=MESH).start()
+    md_recv[depth] = packed
+    wait_bytes(md_recv.at[pl.ds(0, ring - 1)], recv_sem.at[5])
     packed = jnp.sum(md_recv[...], axis=0) * (1.0 / (count * no * nx * ny * nz))
 
     cross, image, older_image, own, mixed, older = [
@@ -316,7 +384,8 @@
 
     def scale(n, carry):
         i, p = lax.div(n, planes), lax.rem(n, planes)
-        value = img[i, p] - cross * cur[i, p].astype(F32) - beta_now * pre[i, p].astype(F32)
+        value = img[i, p] + orb[i, p].astype(F32) * potential[p]
+        value = value - cross * cur[i, p].astype(F32) - beta_now * pre[i, p].astype(F32)
         out[i, p] = (value * inverse).astype(BF16)
         return carry
 
@@ -325,8 +394,8 @@
     wait_bytes(a_send.at[pl.ds(0, nd - 1)], send_sem.at[1])
     wait_bytes(b_send.at[pl.ds(0, nd - 1)], send_sem.at[2])
     wait_bytes(g_recv.at[pl.ds(0, no - 1)], send_sem.at[3])
-    wait_bytes(mo_recv.at[pl.ds(0, no - 1)], send_sem.at[4])
-    wait_bytes(md_recv.at[pl.ds(0, nd - 1)], send_sem.at[5])
+    wait_bytes(mo_recv.at[pl.ds(0, 4 * no - 1)], send_sem.at[4])
+    wait_bytes(md_recv.at[pl.ds(0, ring - 1)], send_sem.at[5])
 
 
 def per_device(nd, no, orbitals, energies, local_potential, lanczos, previous, beta):
@@ -363,11 +432,13 @@
             vmem((nd, 2, nz), BF16), vmem((nd, 2, nz), BF16),
             vmem((nd, 2, nz), BF16), vmem((nd, 2, nz), BF16),
             vmem((planes, rows, nz), BF16), vmem((no, planes, rows, nz), BF16),
-            vmem((1, nz), F32), vmem((no, 1, nz), F32),
-            vmem((1, nz), F32), vmem((nd, 1, nz), F32),
-            vmem((3, 8, nz), F32), vmem((nd, 2, nz), F32),
+            vmem((1, nz), F32), vmem((4 * no, 1, nz), F32),
+            vmem((1, nz), F32), vmem((nd // 4, 1, nz), F32),
+            vmem((6, 8, nz), F32), vmem((nd, 2, nz), F32),
+            vmem((4, *field[1:]), F32), vmem(field[1:], F32),
             pltpu.SMEM((count,), F32), pltpu.SMEM((1,), F32),
             dma((9,)), dma((4,)), dma((6,)), dma((6,)), dma((planes,)),
+            pltpu.SemaphoreType.REGULAR((4,)), pltpu.SemaphoreType.REGULAR(()),
         ],
         compiler_params=pltpu.CompilerParams(collective_id=0, has_side_effects=True),
     )(energies, beta, orbitals, local_potential, lanczos, previous,

time: 64.5 us -> 64 us (level)
  no operation moved by 1% of the time
where the time goes in v3:
time: 64 us; the launch traced here: 63.9 us
  Pallas kernels  58.3 us (91%)
  between operations  4.74 us (7%)
  local copies, waits for them, and re-layouts  0.8 us (1%)
    pallas_call x1, Pallas kernels, per_device(): pl.pallas_call(functools.partial(kernel, nd, no), out_shape=(pltpu.VMEM(f...  58.3 us

profile of v3, /device:TPU:1, one launch (start us, length us, event | category | flops | bytes accessed | tf_op | source)
XLA Modules:
  0.0 63.9 jit_solution(3106159899672365857)
XLA Ops:
  1.3 58.3 %shard_map.112 = (bf16[2,4,256,128]{3,2,1,0:T(8,128)(2,1)S(1)}, f32[1]{0:T(128)}, f32[1]{0:T(128)}) custom-call(f32[2]{0:T(128)} %energies_hbm.1, f32[1]{0:T(128)S(6)} %copy.16.beta_hbm, bf16[2,4,256,128]{3,2,1,0:T(8,128)(2,1)} %orb_hbm.1, f32[4,256,128]{2,1,0:T(8,128)} %loc_hbm.1, bf16[2,4,256,128]{3,2,1,0:T(8,128)(2,1)} %cur_hbm.1, ...), custom_call_target="tpu_custom_call" | custom-call | tf_op jit(solution)/shard_map/pallas_call | solution.py:417
  59.6 0.8 %copy.15 = bf16[2,4,256,128]{3,2,1,0:T(8,128)(2,1)} copy(bf16[2,4,256,128]{3,2,1,0:T(8,128)(2,1)S(1)} %get-tuple-element.3) | data formatting | bytes 1048576

commit v4 on v3

--- a/solution.py
+++ b/solution.py
@@ -131,14 +131,24 @@
         load.wait()
     cz = (t128[0], t128[1])
 
-    def forward(p, carry):
-        field = jnp.zeros((ny, nz), F32)
-        for i in range(count):
-            field = field + orb[i, p].astype(F32) * cur[i, p].astype(F32)
-        field = dot3(split(field), cz)
-        field = dot3((ty[0], ty[1]), split(field))
-        rs_send[:, p] = field.reshape(no, rows, nz).astype(BF16)
-        return carry
+    def across(fields):
+        return jnp.concatenate(fields, axis=1)
+
+    def stacked(field):
+        return jnp.concatenate([field[:, :nz], field[:, nz:]], axis=0)
+
+    def forward(p):
+        fields = []
+        for n in range(2):
+            field = jnp.zeros((ny, nz), F32)
+            for i in range(count):
+                field = field + orb[i, p + n].astype(F32) * cur[i, p + n].astype(F32)
+            fields.append(field)
+        field = dot3(split(jnp.concatenate(fields, axis=0)), cz)
+        field = dot3((ty[0], ty[1]), split(across([field[:ny], field[ny:]])))
+        for n in range(2):
+            part = field[:, n * nz : (n + 1) * nz]
+            rs_send[:, p + n] = part.reshape(no, rows, nz).astype(BF16)
 
     def spread(n, stride):
         tell(heard.at[n], along(stride))
@@ -152,15 +162,13 @@
             rs_send.at[j, p], rs_recv.at[mine, p], send_sem.at[0], recv_sem.at[0],
             device_id={"orb": j}, device_id_type=MESH).start())
 
-    first = planes // 2
-    lax.fori_loop(0, first, forward, 0)
-    pl.semaphore_wait(barrier, no + 5)
-    spread(0, strides[0])
-    for p in range(first):
+    for p in range(0, planes, 2):
+        forward(p)
+        if p == 0:
+            pl.semaphore_wait(barrier, no + 5)
+            spread(0, strides[0])
         scatter(p)
-    for p in range(first, planes):
-        forward(p, 0)
-        scatter(p)
+        scatter(p + 1)
     upward = pltpu.make_async_remote_copy(
         cur.at[:, pl.ds(planes - 3, 3)], below, near_sem.at[0], near_sem.at[1],
         device_id={"dom": lax.rem(me + 1, nd)}, device_id_type=MESH)
@@ -171,13 +179,14 @@
     top = lax.rem(me, turn) == turn - 1
     bottom = lax.rem(me, turn) == 0
 
-    @pl.when(jnp.logical_not(top))
-    def _():
-        upward.start()
-
-    @pl.when(jnp.logical_not(bottom))
-    def _():
-        downward.start()
+    def inner_halo():
+        @pl.when(jnp.logical_not(top))
+        def _():
+            upward.start()
+
+        @pl.when(jnp.logical_not(bottom))
+        def _():
+            downward.start()
 
     rs_recv[mine] = rs_send[mine]
 
@@ -210,6 +219,8 @@
         pl.semaphore_wait(heard.at[n], 2)
         if n + 1 < len(strides):
             spread(n + 1, strides[n + 1])
+        if n == max(0, len(strides) - 2):
+            inner_halo()
     for c in chips:
         tell(all_heard, beside(*c))
     for n in range(3):
@@ -328,19 +339,22 @@
             device_id={"orb": j}, device_id_type=MESH).start())
     g_recv[mine] = g_send[...]
 
-    def finish(p, sums):
-        wait_bytes(g_recv.at[pl.ds(0, no - 1), p], plane_sem.at[p])
-        field = g_recv[:, p].reshape(ny, nz)
+    late = (early[3], early[4], early[5])
+    for p in range(0, planes, 2):
+        for n in range(2):
+            wait_bytes(g_recv.at[pl.ds(0, no - 1), p + n], plane_sem.at[p + n])
+        field = across([g_recv[:, p + n].reshape(ny, nz) for n in range(2)])
         field = dot(ty[0], field) + dot(ty[1], field)
-        field = dot3(split(field), cz)
-        potential[p] = field
-        return (
-            sums[0] + folded(mixed_fields[0, p] * field),
-            sums[1] + folded((mixed_fields[2, p] + mixed_fields[3, p] * field) * field),
-            sums[2] + folded(mixed_fields[1, p] * field),
-        )
-
-    late = lax.fori_loop(0, planes, finish, (early[3], early[4], early[5]))
+        field = dot3(split(stacked(field)), cz)
+        for n in range(2):
+            part = field[n * ny : (n + 1) * ny]
+            potential[p + n] = part
+            late = (
+                late[0] + folded(mixed_fields[0, p + n] * part),
+                late[1] + folded((mixed_fields[2, p + n] + mixed_fields[3, p + n] * part) * part),
+                late[2] + folded(mixed_fields[1, p + n] * part),
+            )
+
     ones = lax.broadcasted_iota(jnp.int32, (1, nz), 1)
 
     def whole(value):
@@ -409,7 +423,6 @@
     t128 = np.stack(high_low(cas_table(nz)) + high_low(side_table(nz, central_weight)))
     ty = np.stack(high_low(cas_table(ny)) + high_low(side_table(ny, 2.0 * central_weight)))
     tx = np.stack(high_low(cas_x[:, order]) + high_low(cas_x[order, :]))
-    hbm = pl.BlockSpec(memory_space=pl.ANY)
     smem = pl.BlockSpec(memory_space=pltpu.SMEM)
     vmem = pltpu.VMEM
     field = (count, planes, ny, nz)
@@ -418,10 +431,10 @@
         functools.partial(kernel, nd, no),
         out_shape=(
             pltpu.VMEM(field, BF16),
-            jax.ShapeDtypeStruct((1,), F32),
-            jax.ShapeDtypeStruct((1,), F32),
+            pltpu.SMEM((1,), F32),
+            pltpu.SMEM((1,), F32),
         ),
-        in_specs=[hbm] * 9,
+        in_specs=[pl.BlockSpec(memory_space=pltpu.HBM)] * 9,
         out_specs=(pl.BlockSpec(memory_space=vmem), smem, smem),
         scratch_shapes=[
             vmem(field, BF16), vmem(field[1:], F32), vmem(field, BF16), vmem(field, BF16),

time: 64 us -> 61.1 us (0.955)
  between operations: 4.74 us -> 2.32 us
where the time goes in v4:
time: 61.1 us; the launch traced here: 61 us
  Pallas kernels  57.9 us (95%)
  between operations  2.32 us (4%)
  local copies, waits for them, and re-layouts  0.8 us (1%)
    pallas_call x1, Pallas kernels, per_device(): pl.pallas_call(functools.partial(kernel, nd, no), out_shape=(pltpu.VMEM(f...  57.9 us

profile of v4, /device:TPU:1, one launch (start us, length us, event | category | flops | bytes accessed | tf_op | source)
XLA Modules:
  0.0 61.0 jit_solution(17937462987666810217)
XLA Ops:
  1.3 57.9 %shard_map.112 = (bf16[2,4,256,128]{3,2,1,0:T(8,128)(2,1)S(1)}, f32[1]{0:T(128)S(4)}, f32[1]{0:T(128)S(4)}) custom-call(f32[2]{0:T(128)} %energies_hbm.1, f32[1]{0:T(128)S(6)} %copy.18.beta_hbm, bf16[2,4,256,128]{3,2,1,0:T(8,128)(2,1)} %orb_hbm.1, f32[4,256,128]{2,1,0:T(8,128)} %loc_hbm.1, bf16[2,4,256,128]{3,2,1,0:T(8,128)(2,1)} %cur_hbm.1, ...), custom_call_target="tpu_custom_call" | custom-call | tf_op jit(solution)/shard_map/pallas_call | solution.py:430
  60.2 0.8 %copy.15 = bf16[2,4,256,128]{3,2,1,0:T(8,128)(2,1)} copy(bf16[2,4,256,128]{3,2,1,0:T(8,128)(2,1)S(1)} %get-tuple-element.3) | data formatting | bytes 1048576

commit v5 on v4

--- a/solution.py
+++ b/solution.py
@@ -102,7 +102,7 @@
             (energies_hbm, energies), (beta_hbm, beta),
         ))
     ]
-    for load in loads:
+    for load in loads[:4]:
         load.start()
     ring = nd // 4
     core = lax.rem(me, 2)
@@ -124,11 +124,17 @@
     barrier = pltpu.get_barrier_semaphore()
     cyclic(mine, no, lambda j: pl.semaphore_signal(
         barrier, inc=1, device_id={"orb": j}, device_id_type=MESH))
-    for j in [beside(*c) for c in chips] + [along(1), along(-1), outer]:
+    near = ring // 4
+    for step in range(near, 0, -1):
+        tell(barrier, along(step))
+        tell(barrier, along(-step))
+    for j in [beside(*c) for c in chips] + [outer]:
         tell(barrier, j)
 
     for load in loads[:4]:
         load.wait()
+    for load in loads[4:]:
+        load.start()
     cz = (t128[0], t128[1])
 
     def across(fields):
@@ -150,13 +156,6 @@
             part = field[:, n * nz : (n + 1) * nz]
             rs_send[:, p + n] = part.reshape(no, rows, nz).astype(BF16)
 
-    def spread(n, stride):
-        tell(heard.at[n], along(stride))
-        tell(heard.at[n], along(-stride))
-
-    strides = [1]
-    while 2 * sum(strides, 1) < ring:
-        strides.append(sum(strides, 1))
     def scatter(p):
         cyclic(mine, no, lambda j: pltpu.make_async_remote_copy(
             rs_send.at[j, p], rs_recv.at[mine, p], send_sem.at[0], recv_sem.at[0],
@@ -165,8 +164,9 @@
     for p in range(0, planes, 2):
         forward(p)
         if p == 0:
-            pl.semaphore_wait(barrier, no + 5)
-            spread(0, strides[0])
+            pl.semaphore_wait(barrier, no + 3 + 2 * near)
+            tell(heard, along(near))
+            tell(heard, along(-near))
         scatter(p)
         scatter(p + 1)
     upward = pltpu.make_async_remote_copy(
@@ -179,14 +179,13 @@
     top = lax.rem(me, turn) == turn - 1
     bottom = lax.rem(me, turn) == 0
 
-    def inner_halo():
-        @pl.when(jnp.logical_not(top))
-        def _():
-            upward.start()
-
-        @pl.when(jnp.logical_not(bottom))
-        def _():
-            downward.start()
+    @pl.when(jnp.logical_not(top))
+    def _():
+        upward.start()
+
+    @pl.when(jnp.logical_not(bottom))
+    def _():
+        downward.start()
 
     rs_recv[mine] = rs_send[mine]
 
@@ -211,16 +210,8 @@
         )
 
     zero = jnp.zeros((8, nz), F32)
-    known = (zero, zero, zero)
-    piece = count * planes // len(strides)
-    for n in range(len(strides)):
-        stop = count * planes if n == len(strides) - 1 else (n + 1) * piece
-        known = lax.fori_loop(n * piece, stop, local, known)
-        pl.semaphore_wait(heard.at[n], 2)
-        if n + 1 < len(strides):
-            spread(n + 1, strides[n + 1])
-        if n == max(0, len(strides) - 2):
-            inner_halo()
+    known = lax.fori_loop(0, count * planes, local, (zero, zero, zero))
+    pl.semaphore_wait(heard, 2)
     for c in chips:
         tell(all_heard, beside(*c))
     for n in range(3):
@@ -381,13 +372,21 @@
             md_send, md_recv.at[depth], send_sem.at[5], recv_sem.at[5],
             device_id={"dom": along(step)}, device_id_type=MESH).start()
     md_recv[depth] = packed
+    beta_now = beta[0]
+
+    def ready(n, carry):
+        i, p = lax.div(n, planes), lax.rem(n, planes)
+        value = img[i, p] + orb[i, p].astype(F32) * potential[p]
+        img[i, p] = value - beta_now * pre[i, p].astype(F32)
+        return carry
+
+    lax.fori_loop(0, count * planes, ready, 0)
     wait_bytes(md_recv.at[pl.ds(0, ring - 1)], recv_sem.at[5])
     packed = jnp.sum(md_recv[...], axis=0) * (1.0 / (count * no * nx * ny * nz))
 
     cross, image, older_image, own, mixed, older = [
         jnp.sum(jnp.where(ones == n, packed, 0.0), axis=1, keepdims=True) for n in range(6)
     ]
-    beta_now = beta[0]
     squares = image - 2.0 * cross * cross - 2.0 * beta_now * older_image
     squares = squares + cross * cross * own + 2.0 * cross * beta_now * mixed
     squares = squares + beta_now * beta_now * older
@@ -398,8 +397,7 @@
 
     def scale(n, carry):
         i, p = lax.div(n, planes), lax.rem(n, planes)
-        value = img[i, p] + orb[i, p].astype(F32) * potential[p]
-        value = value - cross * cur[i, p].astype(F32) - beta_now * pre[i, p].astype(F32)
+        value = img[i, p] - cross * cur[i, p].astype(F32)
         out[i, p] = (value * inverse).astype(BF16)
         return carry
 
@@ -410,6 +408,14 @@
     wait_bytes(g_recv.at[pl.ds(0, no - 1)], send_sem.at[3])
     wait_bytes(mo_recv.at[pl.ds(0, 4 * no - 1)], send_sem.at[4])
     wait_bytes(md_recv.at[pl.ds(0, ring - 1)], send_sem.at[5])
+
+
+def emit(*refs):
+    copies = [pltpu.make_async_copy(refs[n], refs[n + 3], refs[6].at[n]) for n in range(3)]
+    for copy in copies:
+        copy.start()
+    for copy in copies:
+        copy.wait()
 
 
 def per_device(nd, no, orbitals, energies, local_potential, lanczos, previous, beta):
@@ -427,7 +433,7 @@
     vmem = pltpu.VMEM
     field = (count, planes, ny, nz)
     dma = pltpu.SemaphoreType.DMA
-    return pl.pallas_call(
+    results = pl.pallas_call(
         functools.partial(kernel, nd, no),
         out_shape=(
             pltpu.VMEM(field, BF16),
@@ -451,11 +457,18 @@
             vmem((4, *field[1:]), F32), vmem(field[1:], F32),
             pltpu.SMEM((count,), F32), pltpu.SMEM((1,), F32),
             dma((9,)), dma((4,)), dma((6,)), dma((6,)), dma((planes,)),
-            pltpu.SemaphoreType.REGULAR((4,)), pltpu.SemaphoreType.REGULAR(()),
+            pltpu.SemaphoreType.REGULAR(()), pltpu.SemaphoreType.REGULAR(()),
         ],
         compiler_params=pltpu.CompilerParams(collective_id=0, has_side_effects=True),
     )(energies, beta, orbitals, local_potential, lanczos, previous,
       jnp.asarray(t128), jnp.asarray(ty), jnp.asarray(tx))
+    return pl.pallas_call(
+        emit,
+        out_shape=tuple(jax.ShapeDtypeStruct(r.shape, r.dtype) for r in results),
+        in_specs=[pl.BlockSpec(memory_space=vmem), smem, smem],
+        out_specs=(pl.BlockSpec(memory_space=pltpu.HBM),) * 3,
+        scratch_shapes=[dma((3,))],
+    )(pltpu.with_memory_space_constraint(results[0], pltpu.VMEM), *results[1:])
 
 
 def solution(mesh):

time: 61.1 us -> 57.5 us (0.941)
  Pallas kernels: 57.9 us -> 56 us
  between operations: 2.32 us -> 1.29 us
  local copies, waits for them, and re-layouts: 0.8 us -> 0 us
    pallas_call x1, Pallas kernels: 57.9 us -> 55.2 us  [per_device(): pl.pallas_call(functools.partial(kernel, nd, no), out_shape=(pltpu.VMEM(f...]
    pallas_call x0 -> x1, Pallas kernels: none -> 0.84 us  [per_device(): pl.pallas_call(emit, out_shape=tuple((jax.ShapeDtypeStruct(r.shape, r.dty...]
    unnamed x1 -> x0, local copies, waits for them, and re-layouts: 0.8 us -> none
where the time goes in v5:
time: 57.5 us; the launch traced here: 57.3 us
  Pallas kernels  56 us (97%)
  between operations  1.29 us (2%)
    pallas_call x1, Pallas kernels, per_device(): pl.pallas_call(functools.partial(kernel, nd, no), out_shape=(pltpu.VMEM(f...  55.2 us

profile of v5, /device:TPU:1, one launch (start us, length us, event | category | flops | bytes accessed | tf_op | source)
XLA Modules:
  0.0 57.3 jit_solution(14118847636801727159)
XLA Ops:
  1.3 55.2 %shard_map.112 = (bf16[2,4,256,128]{3,2,1,0:T(8,128)(2,1)S(1)}, f32[1]{0:T(128)S(4)}, f32[1]{0:T(128)S(4)}) custom-call(f32[2]{0:T(128)} %energies_hbm.1, f32[1]{0:T(128)S(6)} %copy.12.beta_hbm, bf16[2,4,256,128]{3,2,1,0:T(8,128)(2,1)} %orb_hbm.1, f32[4,256,128]{2,1,0:T(8,128)} %loc_hbm.1, bf16[2,4,256,128]{3,2,1,0:T(8,128)(2,1)} %cur_hbm.1, ...), custom_call_target="tpu_custom_call" | custom-call | tf_op jit(solution)/shard_map/pallas_call | solution.py:436
  56.5 0.8 %shard_map.113 = (bf16[2,4,256,128]{3,2,1,0:T(8,128)(2,1)}, f32[1]{0:T(128)}, f32[1]{0:T(128)}) custom-call(bf16[2,4,256,128]{3,2,1,0:T(8,128)(2,1)S(1)} %get-tuple-element.6.refs_0_, f32[1]{0:T(128)S(4)} %get-tuple-element.7.refs_1_, f32[1]{0:T(128)S(4)} %get-tuple-element.8.refs_2_), custom_call_target="tpu_custom_call" | custom-call | tf_op jit(solution)/shard_map/pallas_call | solution.py:465

commit v6 on v5

--- a/solution.py
+++ b/solution.py
@@ -61,19 +61,27 @@
     around(quarter)
     around(3 * quarter)
 
-    def nearer(step, carry):
-        around(quarter + step)
-        around(quarter - step)
-        around(3 * quarter + step)
-        around(3 * quarter - step)
+    block = 3 if (quarter - 1) % 3 == 0 else 1
+
+    def nearer(n, carry):
+        for part in range(block):
+            step = n * block + part + 1
+            around(quarter + step)
+            around(quarter - step)
+            around(3 * quarter + step)
+            around(3 * quarter - step)
         return carry
 
-    lax.fori_loop(1, quarter, nearer, 0)
+    lax.fori_loop(0, (quarter - 1) // block, nearer, 0)
     around(2 * quarter)
 
 
+def far_first(start, size):
+    return sorted(range(start, size), key=lambda n: abs(2 * n - size))
+
+
 def cyclic(me, size, action):
-    for step in range(1, size):
+    for step in far_first(1, size):
         action(lax.rem(me + step, size))
 
 
@@ -356,7 +364,7 @@
         packed = jnp.where(ones == n, whole(value), packed)
     mo_send[...] = packed
     here = mine * 4 + wide_x * 2 + core
-    for step in range(no):
+    for step in far_first(0, no):
         for c in chips + ((0, 0),):
             if step or c != (0, 0):
                 pltpu.make_async_remote_copy(
@@ -367,7 +375,7 @@
     wait_bytes(mo_recv.at[pl.ds(0, 4 * no - 1)], recv_sem.at[4])
     packed = jnp.sum(mo_recv[...], axis=0)
     md_send[...] = packed
-    for step in sorted(range(1, ring), key=lambda n: abs(2 * n - ring)):
+    for step in far_first(1, ring):
         pltpu.make_async_remote_copy(
             md_send, md_recv.at[depth], send_sem.at[5], recv_sem.at[5],
             device_id={"dom": along(step)}, device_id_type=MESH).start()

time: 57.5 us -> 57.4 us (level)
  no operation moved by 1% of the time
where the time goes in v6:
time: 57.4 us; the launch traced here: 57.2 us
  Pallas kernels  55.9 us (97%)
  between operations  1.29 us (2%)
    pallas_call x1, Pallas kernels, per_device(): pl.pallas_call(functools.partial(kernel, nd, no), out_shape=(pltpu.VMEM(f...  55.1 us

profile of v6, /device:TPU:1, one launch (start us, length us, event | category | flops | bytes accessed | tf_op | source)
XLA Modules:
  0.0 57.2 jit_solution(17750384051159541955)
XLA Ops:
  1.3 55.1 %shard_map.112 = (bf16[2,4,256,128]{3,2,1,0:T(8,128)(2,1)S(1)}, f32[1]{0:T(128)S(4)}, f32[1]{0:T(128)S(4)}) custom-call(f32[2]{0:T(128)} %energies_hbm.1, f32[1]{0:T(128)S(6)} %copy.12.beta_hbm, bf16[2,4,256,128]{3,2,1,0:T(8,128)(2,1)} %orb_hbm.1, f32[4,256,128]{2,1,0:T(8,128)} %loc_hbm.1, bf16[2,4,256,128]{3,2,1,0:T(8,128)(2,1)} %cur_hbm.1, ...), custom_call_target="tpu_custom_call" | custom-call | tf_op jit(solution)/shard_map/pallas_call | solution.py:444
  56.4 0.8 %shard_map.113 = (bf16[2,4,256,128]{3,2,1,0:T(8,128)(2,1)}, f32[1]{0:T(128)}, f32[1]{0:T(128)}) custom-call(bf16[2,4,256,128]{3,2,1,0:T(8,128)(2,1)S(1)} %get-tuple-element.6.refs_0_, f32[1]{0:T(128)S(4)} %get-tuple-element.7.refs_1_, f32[1]{0:T(128)S(4)} %get-tuple-element.8.refs_2_), custom_call_target="tpu_custom_call" | custom-call | tf_op jit(solution)/shard_map/pallas_call | solution.py:473
